TPU v7x, 256 devices: a 8x8x2 block of a 8x8x16 slice. The times are simulated.
256 devices in a mesh: groups: 2 (over z), steps: 128 (over y, x, core).
Axes of the slice: x: 8, y: 8, z: 2, core: 2. Of those that a mesh axis runs over, the one named last changes fastest.
The devices are a block of a 8x8x16 slice.
Arguments:
- states: float32 [256, 4, 4096], P(('groups', 'steps')), parts along dimension 0, may hold values from -6 to 6
- t_sched: int32 [514], P('groups'), parts along dimension 0, may hold values from 0 to 999, as said below
- advances: int32 [4], P('groups'), parts along dimension 0, may hold values from 1 to 128, as said below
- in_weight: bfloat16 [320, 4], replicated, may hold values from -3 to 3
- time_weight: float32 [320, 320], replicated, may hold values from -0.3125 to 0.3125
- mid_weight: bfloat16 [320, 320], replicated, may hold values from -0.3125 to 0.3125
- out_weight: bfloat16 [4, 320], replicated, may hold values from -0.3125 to 0.3125
Outputs:
- final_states: float32 [256, 4, 4096], P(('groups', 'steps')), parts along dimension 0
- errors: float32 [4, 4, 128], P('groups', None, 'steps'), parts along dimension 0
There are 2 independent parts, one for each index of `groups`. A program takes and returns all parts, laid end to end along the dimension named above; an argument that names none is the same for every part. Nothing has to cross between parts.
Inputs may be any that keep to these rules, and one draw needn't show every extreme that they name: `t_sched`: strictly decreasing. Some round advances by exactly 128.
All inputs are finite; a program needn't handle non-finite values.
Results may differ from a plain program's by a relative error of at most 0.0024.
Values sent between devices are 32-bit elements; how exact they have to be, the bound alone decides.
No kernel may reach another device: no remote copies, remote signals or barrier semaphores. Data moves between devices by JAX's collectives and lax.ppermute only.
A program may use at most 64 MiB of HBM per device.

v0:
```python
import math

import jax
import jax.numpy as jnp
from jax import lax
from jax.sharding import Mesh
from jax.sharding import PartitionSpec as P

TSTEPS = 1000
ITERS = 4
ROUNDS = 2
STEPS = ("steps_0", "steps_1", "steps_2")
GROUPS_STEPS = ("groups", "steps_0", "steps_1", "steps_2")


def neutral_like(value, identity):
    return jnp.zeros_like(value) + jnp.asarray(identity, value.dtype)


def entering(value, axes, combine, identity):
    before = start = neutral_like(value, identity)
    so_far = value
    for axis in reversed(axes):
        devices, place = (lax.axis_size(axis), lax.axis_index(axis))
        pieces = lax.all_gather(so_far, axis)
        inside, so_far = (start, start)
        for k in range(devices):
            passed = k < place
            so_far = combine(so_far, pieces[k])
            inside = jnp.where(passed, so_far, inside)
        before = combine(inside, before)
    return before


def alpha_table():
    levels = jnp.arange(TSTEPS, dtype=jnp.float32)
    low = math.sqrt(0.00085)
    high = math.sqrt(0.012)
    betas = (low + (high - low) * levels / (TSTEPS - 1)) ** 2
    return jnp.exp(jnp.cumsum(jnp.log1p(-betas)))


def time_features(stamp, width):
    halfwidth = width // 2
    freqs = jnp.exp(-math.log(10000.0) * jnp.arange(halfwidth, dtype=jnp.float32) / halfwidth)
    angles = stamp.astype(jnp.float32) * freqs
    return jnp.concatenate([jnp.cos(angles), jnp.sin(angles)])


def lookup(alphas, stamp):
    levels = jnp.arange(alphas.shape[0], dtype=jnp.int32)
    return jnp.sum(jnp.where(levels == stamp, alphas, 0.0))


def denoise(state, embed, in_weight, mid_weight, out_weight):
    pre = (
        jnp.dot(in_weight, state.astype(jnp.bfloat16), preferred_element_type=jnp.float32)
        + embed[:, None]
    )
    hidden_one = jax.nn.silu(pre).astype(jnp.bfloat16)
    mixed = jnp.dot(mid_weight, hidden_one, preferred_element_type=jnp.float32)
    hidden_two = (jax.nn.silu(mixed) + pre).astype(jnp.bfloat16)
    return jnp.dot(out_weight, hidden_two, preferred_element_type=jnp.float32)


def add_terms(earlier, later):
    return earlier + later


def shards(states, t_sched, advances, in_weight, time_weight, mid_weight, out_weight):
    window = lax.axis_size(STEPS)
    own_index = lax.axis_index(STEPS)
    alphas = alpha_table()
    current = states
    window_start = jnp.int32(0)
    error_rows = []
    for round_no in range(ROUNDS):
        stamp_now = lax.dynamic_slice_in_dim(t_sched, window_start + own_index, 1)[0]
        stamp_next = lax.dynamic_slice_in_dim(t_sched, window_start + own_index + 1, 1)[0]
        alpha_now = lookup(alphas, stamp_now)
        alpha_next = lookup(alphas, stamp_next)
        coef_one = jnp.sqrt(alpha_next / alpha_now)
        coef_two = jnp.sqrt(1.0 - alpha_next) - coef_one * jnp.sqrt(1.0 - alpha_now)
        feats = time_features(stamp_now, time_weight.shape[1])
        embed = jnp.dot(time_weight, feats, precision=lax.Precision.HIGHEST)
        is_first = own_index == 0
        sweep_rows = []
        for sweep in range(ITERS):
            noise = denoise(current[0], embed, in_weight, mid_weight, out_weight)
            drift = (coef_one - 1.0) * current + coef_two * noise[None]
            term = drift + jnp.where(is_first, current, 0.0)
            prefix = entering(term, STEPS, add_terms, jnp.zeros_like(term))
            updated = jnp.where(is_first, current, prefix)
            sweep_rows.append(jnp.mean((updated - current) ** 2))
            current = updated
        error_rows.append(jnp.stack(sweep_rows))
        advance = advances[round_no]
        target = own_index + advance
        wanted = jnp.minimum(target, window - 1)
        block = lax.all_gather(current, STEPS, axis=0, tiled=True)
        row_ids = jnp.arange(block.shape[0], dtype=jnp.int32)
        selected = jnp.where((row_ids == wanted)[:, None, None], block, 0.0)
        current = jnp.zeros_like(current) + jnp.sum(selected, axis=0, keepdims=True)
        window_start = window_start + advance
    errors = jnp.stack(error_rows).reshape(ROUNDS, ITERS, 1)
    return (current, errors)


def solution(mesh):
    split = Mesh(
        mesh.devices.reshape(mesh.shape["groups"], 8, 8, 2),
        ("groups", "steps_0", "steps_1", "steps_2"),
    )
    in_specs = (P(GROUPS_STEPS, None, None), P("groups"), P("groups"), P(), P(), P(), P())
    out_specs = (P(GROUPS_STEPS, None, None), P("groups", None, STEPS))
    return jax.shard_map(
        shards, mesh=split, in_specs=in_specs, out_specs=out_specs, check_vma=False
    )
```

profile of v0, /device:TPU:513, one launch (start us, length us, event | category | flops | bytes accessed | tf_op | source)
XLA Modules:
  0.0 739.6 jit_solution(762342680965915315)
XLA Ops:
  7.3 1.3 fusion.169
  9.3 1.5 fusion.168
  12.1 3.1 select_reduce_fusion.2
  18.7 4.2 convolution_add_fusion.7
  22.9 7.5 %fusion.34 = f32[1,4,4096]{2,1,0:T(4,128)S(1)} fusion(bf16[4,320]{1,0:T(4,128)(2,1)S(1)} %copy-done.5, f32[320,4096]{1,0:T(8,128)} %convolution_add_fusion.7, bf16[320,320]{1,0:T(8,128)(2,1)S(1)} %copy-done.4, f32[1,4,4096]{2,1,0:T(4,128)S(1)} %copy-done.2, f32[]{:T(128)S(6)} %sub.69, f32[]{:T(128)S(6)} %sub.66, pred[]{:T(512)S(6)} %eq.50), kind=kOutput, calls=%fused_computation.76 | convolution fusion | flops 863846400 | bytes 5581321 | tf_op jit(solution)/shard_map/dot_general | solution.py:63
  30.4 22.0 %all-gather = f32[2,4,4096]{2,1,0:T(4,128)S(1)} all-gather(f32[1,4,4096]{2,1,0:T(4,128)S(1)} %fusion.34), channel_id=2, replica_groups=mesh['groups'=2,'steps_0'=8,'steps_1'=8,'steps_2'=2] {'steps_2'}, dimensions={0}, use_global_device_ids=true | all-gather | bytes 196608 | tf_op jit(solution)/shard_map/all_gather | solution.py:25
  52.5 19.3 %all-gather.8 = f32[8,4,4096]{2,1,0:T(4,128)S(1)} all-gather(f32[1,4,4096]{2,1,0:T(4,128)S(1)} %slice_add_fusion.95), channel_id=10, replica_groups=mesh['groups'=2,'steps_0'=8,'steps_1'=8,'steps_2'=2] {'steps_1'}, dimensions={0}, use_global_device_ids=true | all-gather | bytes 589824 | tf_op jit(solution)/shard_map/all_gather | solution.py:25
  71.8 19.8 %all_gather.121 = f32[8,1,4,4096]{3,2,1,0:T(4,128)S(1)} all-gather(f32[1,1,4,4096]{3,2,1,0:T(4,128)S(1)} %get-tuple-element.42), channel_id=1, replica_groups=mesh['groups'=2,'steps_0'=8,'steps_1'=8,'steps_2'=2] {'steps_0'}, dimensions={0}, use_global_device_ids=true | all-gather | bytes 589824 | tf_op jit(solution)/shard_map/all_gather | solution.py:25
  91.9 3.2 fusion.6
  95.1 7.5 %fusion.31 = f32[1,4,4096]{2,1,0:T(4,128)S(1)} fusion(bf16[4,320]{1,0:T(4,128)(2,1)S(1)} %copy-done.5, f32[320,4096]{1,0:T(8,128)} %fusion.6, bf16[320,320]{1,0:T(8,128)(2,1)S(1)} %copy-done.4, f32[1,4,4096]{2,1,0:T(4,128)S(1)} %fusion.97, f32[]{:T(128)S(6)} %sub.69, f32[]{:T(128)S(6)} %sub.66, pred[]{:T(512)S(6)} %eq.50), kind=kOutput, calls=%fused_computation.72 | convolution fusion | flops 863846400 | bytes 5581321 | tf_op jit(solution)/shard_map/dot_general | solution.py:63
  102.6 13.9 %all-gather.1 = f32[2,4,4096]{2,1,0:T(4,128)S(1)} all-gather(f32[1,4,4096]{2,1,0:T(4,128)S(1)} %fusion.31), channel_id=3, replica_groups=mesh['groups'=2,'steps_0'=8,'steps_1'=8,'steps_2'=2] {'steps_2'}, dimensions={0}, use_global_device_ids=true | all-gather | bytes 196608 | tf_op jit(solution)/shard_map/all_gather | solution.py:25
  116.6 19.3 %all-gather.9 = f32[8,4,4096]{2,1,0:T(4,128)S(1)} all-gather(f32[1,4,4096]{2,1,0:T(4,128)S(1)} %slice_add_fusion.82), channel_id=11, replica_groups=mesh['groups'=2,'steps_0'=8,'steps_1'=8,'steps_2'=2] {'steps_1'}, dimensions={0}, use_global_device_ids=true | all-gather | bytes 589824 | tf_op jit(solution)/shard_map/all_gather | solution.py:25
  135.9 19.3 %all_gather.125 = f32[8,1,4,4096]{3,2,1,0:T(4,128)S(1)} all-gather(f32[1,1,4,4096]{3,2,1,0:T(4,128)S(1)} %get-tuple-element.40), channel_id=1, replica_groups=mesh['groups'=2,'steps_0'=8,'steps_1'=8,'steps_2'=2] {'steps_0'}, dimensions={0}, use_global_device_ids=true | all-gather | bytes 589824 | tf_op jit(solution)/shard_map/all_gather | solution.py:25
  155.4 3.2 fusion.5
  158.6 7.5 %fusion.28 = f32[1,4,4096]{2,1,0:T(4,128)S(1)} fusion(bf16[4,320]{1,0:T(4,128)(2,1)S(1)} %copy-done.5, f32[320,4096]{1,0:T(8,128)} %fusion.5, bf16[320,320]{1,0:T(8,128)(2,1)S(1)} %copy-done.4, f32[1,4,4096]{2,1,0:T(4,128)S(1)} %fusion.90, f32[]{:T(128)S(6)} %sub.69, f32[]{:T(128)S(6)} %sub.66, pred[]{:T(512)S(6)} %eq.50), kind=kOutput, calls=%fused_computation.68 | convolution fusion | flops 863846400 | bytes 5581321 | tf_op jit(solution)/shard_map/dot_general | solution.py:63
  166.1 14.0 %all-gather.2 = f32[2,4,4096]{2,1,0:T(4,128)S(1)} all-gather(f32[1,4,4096]{2,1,0:T(4,128)S(1)} %fusion.28), channel_id=4, replica_groups=mesh['groups'=2,'steps_0'=8,'steps_1'=8,'steps_2'=2] {'steps_2'}, dimensions={0}, use_global_device_ids=true | all-gather | bytes 196608 | tf_op jit(solution)/shard_map/all_gather | solution.py:25
  180.2 19.3 %all-gather.10 = f32[8,4,4096]{2,1,0:T(4,128)S(1)} all-gather(f32[1,4,4096]{2,1,0:T(4,128)S(1)} %slice_add_fusion.69), channel_id=12, replica_groups=mesh['groups'=2,'steps_0'=8,'steps_1'=8,'steps_2'=2] {'steps_1'}, dimensions={0}, use_global_device_ids=true | all-gather | bytes 589824 | tf_op jit(solution)/shard_map/all_gather | solution.py:25
  199.6 19.5 %all_gather.129 = f32[8,1,4,4096]{3,2,1,0:T(4,128)S(1)} all-gather(f32[1,1,4,4096]{3,2,1,0:T(4,128)S(1)} %get-tuple-element.38), channel_id=1, replica_groups=mesh['groups'=2,'steps_0'=8,'steps_1'=8,'steps_2'=2] {'steps_0'}, dimensions={0}, use_global_device_ids=true | all-gather | bytes 589824 | tf_op jit(solution)/shard_map/all_gather | solution.py:25
  219.2 3.2 fusion.4
  222.4 7.5 %fusion.25 = f32[1,4,4096]{2,1,0:T(4,128)S(1)} fusion(bf16[4,320]{1,0:T(4,128)(2,1)S(1)} %copy-done.5, f32[320,4096]{1,0:T(8,128)} %fusion.4, bf16[320,320]{1,0:T(8,128)(2,1)S(1)} %copy-done.4, f32[1,4,4096]{2,1,0:T(4,128)S(1)} %fusion.83, f32[]{:T(128)S(6)} %sub.69, f32[]{:T(128)S(6)} %sub.66, pred[]{:T(512)S(6)} %eq.50), kind=kOutput, calls=%fused_computation.64 | convolution fusion | flops 863846400 | bytes 5581321 | tf_op jit(solution)/shard_map/dot_general | solution.py:63
  229.9 14.0 %all-gather.3 = f32[2,4,4096]{2,1,0:T(4,128)S(1)} all-gather(f32[1,4,4096]{2,1,0:T(4,128)S(1)} %fusion.25), channel_id=5, replica_groups=mesh['groups'=2,'steps_0'=8,'steps_1'=8,'steps_2'=2] {'steps_2'}, dimensions={0}, use_global_device_ids=true | all-gather | bytes 196608 | tf_op jit(solution)/shard_map/all_gather | solution.py:25
  244.0 19.5 %all-gather.11 = f32[8,4,4096]{2,1,0:T(4,128)S(1)} all-gather(f32[1,4,4096]{2,1,0:T(4,128)S(1)} %slice_add_fusion.56), channel_id=13, replica_groups=mesh['groups'=2,'steps_0'=8,'steps_1'=8,'steps_2'=2] {'steps_1'}, dimensions={0}, use_global_device_ids=true | all-gather | bytes 589824 | tf_op jit(solution)/shard_map/all_gather | solution.py:25
  263.5 19.3 %all_gather.133 = f32[8,1,4,4096]{3,2,1,0:T(4,128)S(1)} all-gather(f32[1,1,4,4096]{3,2,1,0:T(4,128)S(1)} %get-tuple-element.36), channel_id=1, replica_groups=mesh['groups'=2,'steps_0'=8,'steps_1'=8,'steps_2'=2] {'steps_0'}, dimensions={0}, use_global_device_ids=true | all-gather | bytes 589824 | tf_op jit(solution)/shard_map/all_gather | solution.py:25
  282.8 1.5 multiply_reduce_fusion.6
  288.7 91.7 %all-gather.27.cloned.1.call-done = f32[128,4,4096]{2,1,0:T(4,128)} async-done(((f32[1,4,4096]{2,1,0:T(4,128)}), f32[128,4,4096]{2,1,0:T(4,128)}) %all-gather.27.cloned.1.call-update) | async-done | bytes 8388624 | tf_op jit(solution)/shard_map/all_gather | solution.py:100
  380.4 5.9 select_reduce_fusion.1
  386.3 3.2 fusion.3
  389.5 7.5 %fusion.22 = f32[1,4,4096]{2,1,0:T(4,128)S(1)} fusion(bf16[4,320]{1,0:T(4,128)(2,1)S(1)} %copy-done.5, f32[320,4096]{1,0:T(8,128)} %fusion.3, bf16[320,320]{1,0:T(8,128)(2,1)S(1)} %copy-done.4, f32[4,4096]{1,0:T(4,128)S(1)} %select_reduce_fusion.1, f32[]{:T(128)S(6)} %sub.73, f32[]{:T(128)S(6)} %sub.70, pred[]{:T(512)S(6)} %eq.50), kind=kOutput, calls=%fused_computation.60 | convolution fusion | flops 863846400 | bytes 5581321 | tf_op jit(solution)/shard_map/dot_general | solution.py:63
  397.0 2.0 all-gather.16
  399.0 19.5 %all-gather.17 = f32[8,4,4096]{2,1,0:T(4,128)S(1)} all-gather(f32[1,4,4096]{2,1,0:T(4,128)S(1)} %slice_add_fusion.43), channel_id=14, replica_groups=mesh['groups'=2,'steps_0'=8,'steps_1'=8,'steps_2'=2] {'steps_1'}, dimensions={0}, use_global_device_ids=true | all-gather | bytes 589824 | tf_op jit(solution)/shard_map/all_gather | solution.py:25
  418.6 20.1 %all_gather.138 = f32[8,1,4,4096]{3,2,1,0:T(4,128)S(1)} all-gather(f32[1,1,4,4096]{3,2,1,0:T(4,128)S(1)} %get-tuple-element.34), channel_id=1, replica_groups=mesh['groups'=2,'steps_0'=8,'steps_1'=8,'steps_2'=2] {'steps_0'}, dimensions={0}, use_global_device_ids=true | all-gather | bytes 589824 | tf_op jit(solution)/shard_map/all_gather | solution.py:25
  438.9 3.2 fusion.2
  442.1 7.5 %fusion.18 = f32[1,4,4096]{2,1,0:T(4,128)S(1)} fusion(bf16[4,320]{1,0:T(4,128)(2,1)S(1)} %copy-done.5, f32[320,4096]{1,0:T(8,128)} %fusion.2, bf16[320,320]{1,0:T(8,128)(2,1)S(1)} %copy-done.4, f32[4,4096]{1,0:T(4,128)S(1)} %get-tuple-element.32, f32[]{:T(128)S(6)} %sub.73, f32[]{:T(128)S(6)} %sub.70, pred[]{:T(512)S(6)} %eq.50), kind=kOutput, calls=%fused_computation.55 | convolution fusion | flops 863846400 | bytes 5581321 | tf_op jit(solution)/shard_map/dot_general | solution.py:63
  449.6 13.5 %all-gather.18 = f32[2,4,4096]{2,1,0:T(4,128)S(1)} all-gather(f32[1,4,4096]{2,1,0:T(4,128)S(1)} %fusion.18), channel_id=7, replica_groups=mesh['groups'=2,'steps_0'=8,'steps_1'=8,'steps_2'=2] {'steps_2'}, dimensions={0}, use_global_device_ids=true | all-gather | bytes 196608 | tf_op jit(solution)/shard_map/all_gather | solution.py:25
  463.2 19.3 %all-gather.19 = f32[8,4,4096]{2,1,0:T(4,128)S(1)} all-gather(f32[1,4,4096]{2,1,0:T(4,128)S(1)} %slice_add_fusion.32), channel_id=15, replica_groups=mesh['groups'=2,'steps_0'=8,'steps_1'=8,'steps_2'=2] {'steps_1'}, dimensions={0}, use_global_device_ids=true | all-gather | bytes 589824 | tf_op jit(solution)/shard_map/all_gather | solution.py:25
  482.5 19.8 %all_gather.142 = f32[8,1,4,4096]{3,2,1,0:T(4,128)S(1)} all-gather(f32[1,1,4,4096]{3,2,1,0:T(4,128)S(1)} %get-tuple-element.30), channel_id=1, replica_groups=mesh['groups'=2,'steps_0'=8,'steps_1'=8,'steps_2'=2] {'steps_0'}, dimensions={0}, use_global_device_ids=true | all-gather | bytes 589824 | tf_op jit(solution)/shard_map/all_gather | solution.py:25
  502.5 3.2 fusion.1
  505.7 7.5 %fusion.14 = f32[1,4,4096]{2,1,0:T(4,128)S(1)} fusion(bf16[4,320]{1,0:T(4,128)(2,1)S(1)} %copy-done.5, f32[320,4096]{1,0:T(8,128)} %fusion.1, bf16[320,320]{1,0:T(8,128)(2,1)S(1)} %copy-done.4, f32[4,4096]{1,0:T(4,128)S(1)} %get-tuple-element.28, f32[]{:T(128)S(6)} %sub.73, f32[]{:T(128)S(6)} %sub.70, pred[]{:T(512)S(6)} %eq.50), kind=kOutput, calls=%fused_computation.50 | convolution fusion | flops 863846400 | bytes 5581321 | tf_op jit(solution)/shard_map/dot_general | solution.py:63
  513.2 14.0 %all-gather.20 = f32[2,4,4096]{2,1,0:T(4,128)S(1)} all-gather(f32[1,4,4096]{2,1,0:T(4,128)S(1)} %fusion.14), channel_id=8, replica_groups=mesh['groups'=2,'steps_0'=8,'steps_1'=8,'steps_2'=2] {'steps_2'}, dimensions={0}, use_global_device_ids=true | all-gather | bytes 196608 | tf_op jit(solution)/shard_map/all_gather | solution.py:25
  527.2 19.7 %all-gather.21 = f32[8,4,4096]{2,1,0:T(4,128)S(1)} all-gather(f32[1,4,4096]{2,1,0:T(4,128)S(1)} %slice_add_fusion.21), channel_id=16, replica_groups=mesh['groups'=2,'steps_0'=8,'steps_1'=8,'steps_2'=2] {'steps_1'}, dimensions={0}, use_global_device_ids=true | all-gather | bytes 589824 | tf_op jit(solution)/shard_map/all_gather | solution.py:25
  547.0 19.5 %all_gather.146 = f32[8,1,4,4096]{3,2,1,0:T(4,128)S(1)} all-gather(f32[1,1,4,4096]{3,2,1,0:T(4,128)S(1)} %get-tuple-element.26), channel_id=1, replica_groups=mesh['groups'=2,'steps_0'=8,'steps_1'=8,'steps_2'=2] {'steps_0'}, dimensions={0}, use_global_device_ids=true | all-gather | bytes 589824 | tf_op jit(solution)/shard_map/all_gather | solution.py:25
  566.6 3.2 fusion
  569.8 7.5 %fusion.10 = f32[1,4,4096]{2,1,0:T(4,128)S(1)} fusion(bf16[4,320]{1,0:T(4,128)(2,1)S(1)} %copy-done.5, f32[320,4096]{1,0:T(8,128)} %fusion, bf16[320,320]{1,0:T(8,128)(2,1)S(1)} %copy-done.4, f32[4,4096]{1,0:T(4,128)S(1)} %get-tuple-element.24, f32[]{:T(128)S(6)} %sub.73, f32[]{:T(128)S(6)} %sub.70, pred[]{:T(512)S(6)} %eq.50), kind=kOutput, calls=%fused_computation.45 | convolution fusion | flops 863846400 | bytes 5581321 | tf_op jit(solution)/shard_map/dot_general | solution.py:63
  577.4 13.7 %all-gather.22 = f32[2,4,4096]{2,1,0:T(4,128)S(1)} all-gather(f32[1,4,4096]{2,1,0:T(4,128)S(1)} %fusion.10), channel_id=9, replica_groups=mesh['groups'=2,'steps_0'=8,'steps_1'=8,'steps_2'=2] {'steps_2'}, dimensions={0}, use_global_device_ids=true | all-gather | bytes 196608 | tf_op jit(solution)/shard_map/all_gather | solution.py:25
  591.1 19.4 %all-gather.23 = f32[8,4,4096]{2,1,0:T(4,128)S(1)} all-gather(f32[1,4,4096]{2,1,0:T(4,128)S(1)} %slice_add_fusion.10), channel_id=17, replica_groups=mesh['groups'=2,'steps_0'=8,'steps_1'=8,'steps_2'=2] {'steps_1'}, dimensions={0}, use_global_device_ids=true | all-gather | bytes 589824 | tf_op jit(solution)/shard_map/all_gather | solution.py:25
  610.6 19.9 %all_gather.150 = f32[8,1,4,4096]{3,2,1,0:T(4,128)S(1)} all-gather(f32[1,1,4,4096]{3,2,1,0:T(4,128)S(1)} %get-tuple-element.22), channel_id=1, replica_groups=mesh['groups'=2,'steps_0'=8,'steps_1'=8,'steps_2'=2] {'steps_0'}, dimensions={0}, use_global_device_ids=true | all-gather | bytes 589824 | tf_op jit(solution)/shard_map/all_gather | solution.py:25
  638.4 87.7 %all-gather.29.cloned.1.call-done = f32[128,4,4096]{2,1,0:T(4,128)} async-done(((f32[1,4,4096]{2,1,0:T(4,128)}), f32[128,4,4096]{2,1,0:T(4,128)}) %all-gather.29.cloned.1.call-update) | async-done | bytes 8388624 | tf_op jit(solution)/shard_map/all_gather | solution.py:100
  726.1 6.5 select_reduce_fusion
  (60 shorter events, 6.4 us)
Async XLA Ops:
  7.2 11.0 %copy-start = (f32[320,320]{1,0:T(8,128)S(1)}, f32[320,320]{1,0:T(8,128)}, u32[]{:S(2)}) copy-start(f32[320,320]{1,0:T(8,128)} %param.11) | copy-start | bytes 1228804
  7.2 15.7 %copy-start.2 = (f32[1,4,4096]{2,1,0:T(4,128)S(1)}, f32[1,4,4096]{2,1,0:T(4,128)}, u32[]{:S(2)}) copy-start(f32[1,4,4096]{2,1,0:T(4,128)} %param.7) | copy-start | bytes 196612
  7.2 15.7 %copy-start.4 = (bf16[320,320]{1,0:T(8,128)(2,1)S(1)}, bf16[320,320]{1,0:T(8,128)(2,1)}, u32[]{:S(2)}) copy-start(bf16[320,320]{1,0:T(8,128)(2,1)} %param.12) | copy-start | bytes 614404
  7.2 15.7 %copy-start.5 = (bf16[4,320]{1,0:T(4,128)(2,1)S(1)}, bf16[4,320]{1,0:T(4,128)(2,1)}, u32[]{:S(2)}) copy-start(bf16[4,320]{1,0:T(4,128)(2,1)} %param.13) | copy-start | bytes 7684
  7.2 373.2 %all-gather.27.cloned.1.call-start = ((), (), s32[]{:S(2)}) async-start(), calls=%async_computation | async-start | bytes 8454144 | tf_op jit(solution)/shard_map/all_gather | solution.py:100
  22.9 69.0 %copy-start.3 = (bf16[320,4]{0,1:T(4,128)(2,1)S(1)}, bf16[320,4]{0,1:T(4,128)(2,1)}, u32[]{:S(2)}) copy-start(bf16[320,4]{0,1:T(4,128)(2,1)} %param.10) | copy-start | bytes 7684
  284.4 441.7 %all-gather.29.cloned.1.call-start = ((), (), s32[]{:S(2)}) async-start(), calls=%async_computation.1 | async-start | bytes 8454144 | tf_op jit(solution)/shard_map/all_gather | solution.py:100
  630.5 102.1 %copy-start.1 = (f32[320,320]{1,0:T(8,128)S(1)}, f32[320,320]{1,0:T(8,128)}, u32[]{:S(2)}) copy-start(f32[320,320]{1,0:T(8,128)} %param.11) | copy-start | bytes 1228804
Sparse Core Ops, SparseCore 0:
  284.5 95.8 all-gather.26
  632.3 93.7 all-gather.28
where the time goes:
time: 748 us; the launch traced here: 740 us
  blocking collectives  420 us (56%)
  waiting for transfers between devices  179 us (24%)
  matrix products  87.9 us (12%)
  between operations  27.5 us (4%)
  other arithmetic  21.6 us (3%)
    all_gather x24, blocking collectives, entering(): pieces = lax.all_gather(so_far, axis)  420 us
    all_gather x2, waiting for transfers between devices, shards(): block = lax.all_gather(current, STEPS, axis=0, tiled=True)  179 us
    dot_general x8, matrix products, denoise(): return jnp.dot(out_weight, hidden_two, preferred_element_type=jnp.float32)  60.2 us
    dot_general x8, matrix products, denoise(): jnp.dot(in_weight, state.astype(jnp.bfloat16), preferred_element_type=jnp...  26.6 us
  transfers between devices with their start and end apart: 2, of which 2 were waited for; matrix products, arithmetic and copies ran while one was open for 0% of the time, Pallas kernels for 0%

commit v1 on v0

v1 whole, which is shorter than its diff:
```python
import functools
import math

import jax
import jax.numpy as jnp
import ml_dtypes
import numpy as np
from jax import lax
from jax.experimental import pallas as pl
from jax.experimental.pallas import tpu as pltpu
from jax.sharding import PartitionSpec as P

TSTEPS = 1000
ITERS = 4
ROUNDS = 2
RADIX = 32
LANES = 128
F32 = jnp.float32
BF16 = jnp.bfloat16


def three_parts(table):
    rest = np.asarray(table, np.float64)
    parts = []
    for _ in range(3):
        part = rest.astype(ml_dtypes.bfloat16)
        parts.append(part)
        rest = rest - part.astype(np.float64)
    return np.concatenate(parts, axis=1)


def tables(width):
    half = width // 2
    freqs = np.exp(-math.log(10000.0) * np.arange(half, dtype=np.float64) / half)
    digits = np.arange(RADIX, dtype=np.float64)
    coarse = freqs[:, None] * (digits * RADIX)[None]
    fine = freqs[:, None] * digits[None]
    levels = np.arange(RADIX * RADIX, dtype=np.float64)
    low, high = math.sqrt(0.00085), math.sqrt(0.012)
    betas = (low + (high - low) * levels / (TSTEPS - 1)) ** 2
    alphas = np.exp(np.cumsum(np.log1p(-betas)))
    root = np.sqrt(alphas).reshape(RADIX, RADIX).T
    rest = np.sqrt(1.0 - alphas).reshape(RADIX, RADIX).T
    table_a = np.concatenate([np.cos(coarse), np.sin(coarse), root, rest], axis=0)
    table_b = np.concatenate([np.cos(fine), np.sin(fine)], axis=0)
    return three_parts(table_a), three_parts(table_b)


def dot(left, right):
    return jnp.dot(left, right, preferred_element_type=F32)


def split2(value):
    high = value.astype(BF16)
    return high, (value - high.astype(F32)).astype(BF16)


def split3(value):
    high = value.astype(BF16)
    rest = value - high.astype(F32)
    mid = rest.astype(BF16)
    return high, mid, (rest - mid.astype(F32)).astype(BF16)


def one_hot(row, count):
    return (lax.broadcasted_iota(jnp.int32, (count, row.shape[1]), 0) == row).astype(F32)


def picard(
    group,
    adv_ref,
    stamps_ref,
    recv_ref,
    in_ref,
    time_ref,
    mid_ref,
    out_w_ref,
    table_a_ref,
    table_b_ref,
    send_ref,
    state,
    embed,
    bias,
    scale_x,
    scale_e,
    mid_half,
    left_in,
    left_out,
    squares,
):
    window, rows = recv_ref.shape
    channels, lat = in_ref.shape
    half = channels // 2
    depth = group * lat
    tiles = rows // depth
    iters = ROUNDS * ITERS

    stamps = stamps_ref[...]
    row = jnp.concatenate([stamps[k : k + 1] for k in (0, 2, 1, 3)], axis=1)
    hot_a = one_hot(row // RADIX, RADIX).astype(BF16)
    digit_b = row % RADIX
    hot_b = one_hot(digit_b, RADIX)
    hot_a3 = jnp.concatenate([hot_a] * 3, axis=0)
    now_b = hot_b[:, : 2 * window].astype(BF16)
    now_b3 = jnp.concatenate([now_b] * 3, axis=0)
    coarse = dot(table_a_ref[: 2 * half, :], hot_a3[:, : 2 * window])
    fine = dot(table_b_ref[...], now_b3)
    roots = dot(table_a_ref[2 * half :, :], hot_a3)
    cos_a, sin_a = coarse[:half], coarse[half:]
    cos_b, sin_b = fine[:half], fine[half:]
    feats = jnp.concatenate([cos_a * cos_b - sin_a * sin_b, sin_a * cos_b + cos_a * sin_b], axis=0)
    temb = jnp.dot(time_ref[...], feats, preferred_element_type=F32, precision=lax.Precision.HIGHEST)
    root = jnp.sum(roots[:RADIX] * hot_b, axis=0, keepdims=True)
    rest = jnp.sum(roots[RADIX:] * hot_b, axis=0, keepdims=True)
    two = 2 * window
    coef_one = root[:, two:] / root[:, :two]
    coef_two = rest[:, two:] - coef_one * rest[:, :two]

    out_w = jnp.concatenate([out_w_ref[...]] * group, axis=0)
    spread = lax.broadcasted_iota(jnp.int32, (lat, depth), 0) == lax.broadcasted_iota(jnp.int32, (lat, depth), 1) % lat
    in_w = dot(in_ref[...], spread.astype(F32).astype(BF16))
    through = dot(out_w, in_w.astype(BF16))
    in_half = (in_w * 0.5).astype(BF16)
    left_in[:channels, :depth] = in_half
    left_in[:channels, depth:] = jnp.zeros_like(in_half)
    high, low = split2(through)
    left_in[channels:, :depth] = high
    left_in[channels:, depth:] = low
    left_out[...] = out_w
    mid_half[...] = (mid_ref[...].astype(F32) * 0.5).astype(BF16)
    parts = split3(temb)
    bias_all = dot(out_w, parts[0]) + dot(out_w, parts[1]) + dot(out_w, parts[2])
    for r in range(ROUNDS):
        lanes = slice(r * window, (r + 1) * window)
        embed[r] = temb[:, lanes] * 0.5
        scale_x[r] = coef_one[:, lanes] - 1.0
        scale_e[r] = coef_two[:, lanes]
        bias[r] = bias_all[:, lanes] * coef_two[:, lanes]

    state[...] = recv_ref[...].T
    squares[...] = jnp.zeros_like(squares)

    earlier = lax.broadcasted_iota(jnp.int32, (window, window), 0)
    later = lax.broadcasted_iota(jnp.int32, (window, window), 1)
    lane_group = lax.broadcasted_iota(jnp.int32, (depth, window), 0) // lat

    def iteration(i, carry):
        r = i // ITERS
        shift = jnp.where(i % ITERS == ITERS - 1, adv_ref[r], 0)
        keep = (earlier < later).astype(F32).astype(BF16)
        moved = (earlier < jnp.minimum(later + shift, window - 1)).astype(F32).astype(BF16)
        sums = jnp.concatenate([keep, moved], axis=1)
        time = embed[r]
        error = jnp.zeros((depth, window), F32)
        for t in range(tiles):
            at = slice(t * depth, (t + 1) * depth)
            x = state[at, :]
            own = [jnp.where(lane_group == g, x, 0.0).astype(BF16) for g in range(group)]
            right = jnp.concatenate(own, axis=1)
            right = jnp.concatenate([right, right], axis=0)
            first = dot(left_in[...], right)
            pre = first[:channels] + jnp.concatenate([time] * group, axis=1)
            hidden = (pre * jnp.tanh(pre) + pre).astype(BF16)
            mixed = dot(mid_half[...], hidden)
            second = (mixed * jnp.tanh(mixed) + mixed).astype(BF16)
            noise = dot(left_out[...], second) + first[channels:]
            picked = noise[:, :window]
            for g in range(1, group):
                picked = jnp.where(lane_group == g, noise[:, g * window : (g + 1) * window], picked)
            drift = scale_x[r] * x + scale_e[r] * picked + bias[r]
            both = sum(dot(part, sums) for part in split3(drift))
            head = x[:, :1]
            change = both[:, :window] + head - x
            error = error + change * change
            state[at, :] = both[:, window:] + head
        squares[pl.ds(i, 1), :] = jnp.sum(error, axis=0, keepdims=True)
        return carry

    lax.fori_loop(0, iters, iteration, 0)
    send_ref[:, :rows] = state[...].T
    send_ref[:, rows:] = squares[...].T


def solve(advances, stamps, received, in_weight, time_weight, mid_weight, out_weight, group):
    window, rows = received.shape
    channels, lat = in_weight.shape
    table_a, table_b = tables(channels)
    depth = group * lat
    vmem = pl.BlockSpec(memory_space=pltpu.VMEM)
    return pl.pallas_call(
        functools.partial(picard, group),
        name="picard",
        out_shape=jax.ShapeDtypeStruct((window, rows + window), F32),
        in_specs=[pl.BlockSpec(memory_space=pltpu.SMEM)] + [vmem] * 8,
        out_specs=vmem,
        scratch_shapes=[
            pltpu.VMEM((rows, window), F32),
            pltpu.VMEM((ROUNDS, channels, window), F32),
            pltpu.VMEM((ROUNDS, depth, window), F32),
            pltpu.VMEM((ROUNDS, 1, window), F32),
            pltpu.VMEM((ROUNDS, 1, window), F32),
            pltpu.VMEM((channels, channels), BF16),
            pltpu.VMEM((channels + depth, 2 * depth), BF16),
            pltpu.VMEM((depth, channels), BF16),
            pltpu.VMEM((window, window), F32),
        ],
    )(advances, stamps, received, in_weight, time_weight, mid_weight, out_weight, jnp.asarray(table_a), jnp.asarray(table_b))


def shards(states, t_sched, advances, in_weight, time_weight, mid_weight, out_weight):
    _, lat, pixels = states.shape
    window = lax.axis_size("steps")
    own = pixels // window
    start = jnp.stack([jnp.int32(0), advances[0]])
    stamps = jnp.stack(
        [lax.dynamic_slice_in_dim(t_sched, start[r] + n, window) for r in range(ROUNDS) for n in range(2)]
    )
    out_going = states[0].reshape(lat, own, window).transpose(2, 1, 0).reshape(window, own * lat)
    received = lax.all_to_all(out_going, "steps", 0, 0, tiled=True)
    send = solve(advances, stamps, received, in_weight, time_weight, mid_weight, out_weight, 4)
    back = lax.all_to_all(send, "steps", 0, 0, tiled=True)
    final = back[:, : own * lat].reshape(window, own, lat).transpose(2, 1, 0).reshape(1, lat, pixels)
    totals = jnp.sum(back[:, own * lat : own * lat + ROUNDS * ITERS], axis=0) / (lat * pixels)
    return final, totals.reshape(ROUNDS, ITERS, 1)


def solution(mesh):
    both = ("groups", "steps")
    in_specs = (P(both, None, None), P("groups"), P("groups"), P(), P(), P(), P())
    out_specs = (P(both, None, None), P("groups", None, "steps"))
    return jax.shard_map(shards, mesh=mesh, in_specs=in_specs, out_specs=out_specs, check_vma=False)
```

time: 748 us -> 111 us (0.15); the launches traced: 740 us -> 111 us
  blocking collectives: 420 us -> 19.8 us
  waiting for transfers between devices: 179 us -> 8.7 us
  matrix products: 87.9 us -> 0 us
  Pallas kernels: 0 us -> 46 us
  starting transfers between devices: 0.34 us -> 27.4 us
  between operations: 27.5 us -> 0.85 us
  other arithmetic: 21.6 us -> 0.72 us
    all_gather x24 -> x0, blocking collectives: 420 us -> none  [entering(): pieces = lax.all_gather(so_far, axis)]
    all_gather x2 -> x0, waiting for transfers between devices: 179 us -> none  [shards(): block = lax.all_gather(current, STEPS, axis=0, tiled=True)]
    dot_general x18 -> x0, matrix products: 87.9 us -> none  [the longest x8 60.2 us: denoise(): return jnp.dot(out_weight, hidden_two, preferred_element_type=jnp.float32)]
    pallas_call x0 -> x1, Pallas kernels: none -> 46 us  [solve(): pl.pallas_call(functools.partial(picard, group), name='picard', out_shape...]
    all_to_all x0 -> x1, starting transfers between devices: none -> 27.4 us  [shards(): received = lax.all_to_all(out_going, 'steps', 0, 0, tiled=True)]
    all_to_all x0 -> x1, blocking collectives: none -> 19.8 us  [shards(): back = lax.all_to_all(send, 'steps', 0, 0, tiled=True)]
    reduce_sum x5 -> x1, other arithmetic: 17.9 us -> 0.11 us  [shards(): jnp.sum(back[:, own * lat:own * lat + ROUNDS * ITERS], axis=0)]
    all_to_all x0 -> x1, waiting for transfers between devices: none -> 8.7 us  [shards(): received = lax.all_to_all(out_going, 'steps', 0, 0, tiled=True)]
  transfers between devices with their start and end apart: 2 -> 1, of which waited for: 2 -> 1; matrix products, arithmetic and copies ran while one was open for 0% -> 1% of each run, Pallas kernels for 0% -> 0%
where the time goes in v1:
time: 111 us
  Pallas kernels  46 us (41%)
  starting transfers between devices  27.4 us (25%)
  blocking collectives  19.8 us (18%)
  waiting for transfers between devices  8.7 us (8%)
  local copies, waits for them, and re-layouts  7.37 us (7%)
    pallas_call x1, Pallas kernels, solve(): pl.pallas_call(functools.partial(picard, group), name='picard', out_shape...  46 us
    all_to_all x1, starting transfers between devices, shards(): received = lax.all_to_all(out_going, 'steps', 0, 0, tiled=True)  27.4 us
    all_to_all x1, blocking collectives, shards(): back = lax.all_to_all(send, 'steps', 0, 0, tiled=True)  19.8 us
    all_to_all x1, waiting for transfers between devices, shards(): received = lax.all_to_all(out_going, 'steps', 0, 0, tiled=True)  8.7 us
    unnamed x9, local copies, waits for them, and re-layouts  3.3 us
  transfers between devices with their start and end apart: 1, of which 1 were waited for; matrix products, arithmetic and copies ran while one was open for 1% of the time, Pallas kernels for 0%

profile of v1, /device:TPU:513, one launch (start us, length us, event | category | flops | bytes accessed | tf_op | source)
XLA Modules:
  0.0 110.9 jit_solution(7658776680701660018)
XLA Ops:
  0.6 1.6 %copy.21 = f32[128,1,128]{2,1,0:T(1,128)} copy(f32[128,1,128]{0,2,1:T(8,128)} %bitcast.28) | data formatting | bytes 131072 | tf_op jit(solution)/shard_map/all_to_all | solution.py:219
  2.2 27.4 %all-to-all-start = ((f32[128,1,128]{2,1,0:T(1,128)}), f32[128,1,128]{2,1,0:T(1,128)S(1)}, u32[]{:S(2)}, u32[]{:S(2)}) async-start(f32[128,1,128]{2,1,0:T(1,128)} %copy.21), calls=%async_computation | async-start | bytes 131072 | tf_op jit(solution)/shard_map/all_to_all | solution.py:219
  29.6 0.0 copy-start.2
  29.6 0.6 copy-done.2
  30.4 0.0 copy-start.3
  30.5 0.6 copy-done.3
  31.1 0.0 copy-start.1
  31.1 0.1 slice_bitcast_fusion.1
  31.2 0.6 copy-done.1
  31.8 0.8 copy.22.in_ref
  32.6 0.6 pad_add_fusion.stamps_ref
  33.2 8.7 %all-to-all-done = f32[128,1,128]{2,1,0:T(1,128)S(1)} async-done(((f32[128,1,128]{2,1,0:T(1,128)}), f32[128,1,128]{2,1,0:T(1,128)S(1)}, u32[]{:S(2)}, u32[]{:S(2)}) %all-to-all-start) | async-done | bytes 65568 | tf_op jit(solution)/shard_map/all_to_all | solution.py:219
  41.9 0.0 copy-start
  41.9 0.6 copy-done
  42.5 46.0 %picard.1 = f32[128,256]{1,0:T(8,128)} custom-call(s32[2]{0:T(128)} %adv_ref.1, s32[4,128]{1,0:T(4,128)} %pad_add_fusion.stamps_ref, f32[128,128]{1,0:T(8,128)} %bitcast.27, bf16[320,4]{1,0:T(8,128)(2,1)} %copy.22.in_ref, f32[320,320]{1,0:T(8,128)} %time_ref.1, bf16[320,320]{1,0:T(8,128)(2,1)} %mid_ref.1, bf16[4,320]{1,0:T(4,128)(2,1)} %out_w_ref.1, ...), custom_call_target="tpu_custom_call" | custom-call | tf_op jit(solution)/shard_map/picard/pallas_call | solution.py:190
  88.5 1.0 copy.23
  89.5 19.8 %all_to_all.23 = f32[128,1,256]{2,1,0:T(1,128)S(1)} all-to-all(f32[128,1,256]{2,1,0:T(1,128)S(1)} %copy.23), channel_id=1, replica_groups=mesh['groups'=2,'steps'=128] {'steps'}, dimensions={0} | all-to-all | bytes 262144 | tf_op jit(solution)/shard_map/all_to_all | solution.py:221
  109.4 0.1 copy.24
  109.5 0.1 slice_reduce_fusion
  109.6 0.6 slice.12
  110.3 0.6 div.6
  (1 shorter events, 0.0 us)
Async XLA Ops:
  2.2 39.7 %all-to-all-start = ((f32[128,1,128]{2,1,0:T(1,128)}), f32[128,1,128]{2,1,0:T(1,128)S(1)}, u32[]{:S(2)}, u32[]{:S(2)}) async-start(f32[128,1,128]{2,1,0:T(1,128)} %copy.21), calls=%async_computation | async-start | bytes 131072 | tf_op jit(solution)/shard_map/all_to_all | solution.py:219
  29.6 0.7 copy-start.2
  30.4 0.7 copy-start.3
  31.1 0.7 copy-start.1
  41.9 0.6 copy-start

commit v2 on v1

v2 whole, which is shorter than its diff:
```python
import functools
import math

import jax
import jax.numpy as jnp
import ml_dtypes
import numpy as np
from jax import lax
from jax.experimental import pallas as pl
from jax.experimental.pallas import tpu as pltpu
from jax.sharding import PartitionSpec as P

TSTEPS = 1000
ITERS = 4
ROUNDS = 2
RADIX = 32
GROUP = 4
LIMIT = 16 * 1024 * 1024
F32 = jnp.float32
BF16 = jnp.bfloat16


def three_parts(table):
    rest = np.asarray(table, np.float64)
    parts = []
    for _ in range(3):
        part = rest.astype(ml_dtypes.bfloat16)
        parts.append(part)
        rest = rest - part.astype(np.float64)
    return np.concatenate(parts, axis=1)


def tables(width):
    half = width // 2
    freqs = np.exp(-math.log(10000.0) * np.arange(half, dtype=np.float64) / half)
    digits = np.arange(RADIX, dtype=np.float64)
    coarse = freqs[:, None] * (digits * RADIX)[None]
    fine = freqs[:, None] * digits[None]
    levels = np.arange(RADIX * RADIX, dtype=np.float64)
    low, high = math.sqrt(0.00085), math.sqrt(0.012)
    betas = (low + (high - low) * levels / (TSTEPS - 1)) ** 2
    alphas = np.exp(np.cumsum(np.log1p(-betas)))
    root = np.sqrt(alphas).reshape(RADIX, RADIX).T
    rest = np.sqrt(1.0 - alphas).reshape(RADIX, RADIX).T
    table_a = np.concatenate([np.cos(coarse), np.sin(coarse), root, rest], axis=0)
    table_b = np.concatenate([np.cos(fine), np.sin(fine)], axis=0)
    return three_parts(table_a), three_parts(table_b)


def dot(left, right):
    return jnp.dot(left, right, preferred_element_type=F32)


def split2(value):
    high = value.astype(BF16)
    return high, (value - high.astype(F32)).astype(BF16)


def split3(value):
    high = value.astype(BF16)
    rest = value - high.astype(F32)
    mid = rest.astype(BF16)
    return high, mid, (rest - mid.astype(F32)).astype(BF16)


def one_hot(row, count):
    return (lax.broadcasted_iota(jnp.int32, (count, row.shape[1]), 0) == row).astype(F32)


def arrange(states_ref, going_ref):
    _, lat, pixels = states_ref.shape
    window = going_ref.shape[0]
    blocks = [states_ref[0, :, p * window : (p + 1) * window] for p in range(pixels // window)]
    going_ref[...] = jnp.concatenate(blocks, axis=0).T


def prepare(
    group,
    adv_ref,
    stamps_ref,
    in_ref,
    time_ref,
    mid_ref,
    out_w_ref,
    table_a_ref,
    table_b_ref,
    embed,
    bias,
    scales,
    limits,
    mid_half,
    left_in,
    left_out,
):
    window = stamps_ref.shape[1]
    channels, lat = in_ref.shape
    half = channels // 2
    depth = group * lat

    stamps = stamps_ref[...]
    row = jnp.concatenate([stamps[k : k + 1] for k in (0, 2, 1, 3)], axis=1)
    hot_a = one_hot(row // RADIX, RADIX).astype(BF16)
    hot_b = one_hot(row % RADIX, RADIX)
    hot_a3 = jnp.concatenate([hot_a] * 3, axis=0)
    now_b = hot_b[:, : ROUNDS * window].astype(BF16)
    now_b3 = jnp.concatenate([now_b] * 3, axis=0)
    coarse = dot(table_a_ref[: 2 * half, :], hot_a3[:, : ROUNDS * window])
    fine = dot(table_b_ref[...], now_b3)
    roots = dot(table_a_ref[2 * half :, :], hot_a3)
    cos_a, sin_a = coarse[:half], coarse[half:]
    cos_b, sin_b = fine[:half], fine[half:]
    feats = jnp.concatenate([cos_a * cos_b - sin_a * sin_b, sin_a * cos_b + cos_a * sin_b], axis=0)
    temb = jnp.dot(time_ref[...], feats, preferred_element_type=F32, precision=lax.Precision.HIGHEST)
    root = jnp.sum(roots[:RADIX] * hot_b, axis=0, keepdims=True)
    rest = jnp.sum(roots[RADIX:] * hot_b, axis=0, keepdims=True)
    now = ROUNDS * window
    coef_one = root[:, now:] / root[:, :now]
    coef_two = rest[:, now:] - coef_one * rest[:, :now]

    out_w = jnp.concatenate([out_w_ref[...]] * group, axis=0)
    spread = lax.broadcasted_iota(jnp.int32, (lat, depth), 0) == lax.broadcasted_iota(jnp.int32, (lat, depth), 1) % lat
    in_w = dot(in_ref[...], spread.astype(F32).astype(BF16))
    through = dot(out_w, in_w.astype(BF16))
    in_half = (in_w * 0.5).astype(BF16)
    left_in[:channels, :depth] = in_half
    left_in[:channels, depth:] = jnp.zeros_like(in_half)
    high, low = split2(through)
    left_in[channels:, :depth] = high
    left_in[channels:, depth:] = low
    left_out[...] = out_w
    mid_half[...] = (mid_ref[...].astype(F32) * 0.5).astype(BF16)
    parts = split3(temb)
    bias_all = dot(out_w, parts[0]) + dot(out_w, parts[1]) + dot(out_w, parts[2])
    place = lax.broadcasted_iota(jnp.int32, (1, window), 1)
    for r in range(ROUNDS):
        lanes = slice(r * window, (r + 1) * window)
        embed[r] = temb[:, lanes] * 0.5
        scales[r, 0:1] = coef_one[:, lanes] - 1.0
        scales[r, 1:2] = coef_two[:, lanes]
        bias[r] = bias_all[:, lanes] * coef_two[:, lanes]
        for k in range(ITERS):
            shift = adv_ref[r] if k == ITERS - 1 else 0
            limits[r * ITERS + k : r * ITERS + k + 1, :] = jnp.minimum(place + shift, window - 1)


def picard(
    group,
    recv_ref,
    embed,
    bias,
    scales,
    limits,
    mid_half,
    left_in,
    left_out,
    send_ref,
    state,
    squares,
    hidden,
    second,
    direct,
):
    window, rows = recv_ref.shape
    channels = mid_half.shape[0]
    depth = left_out.shape[0]
    lat = depth // group
    tiles = rows // depth
    iters = ROUNDS * ITERS

    state[...] = recv_ref[...].T
    squares[...] = jnp.zeros_like(squares)
    earlier = lax.broadcasted_iota(jnp.int32, (window, window), 0)
    later = lax.broadcasted_iota(jnp.int32, (window, window), 1)
    lane_group = lax.broadcasted_iota(jnp.int32, (depth, window), 0) // lat

    def enter(i, t):
        x = state[t * depth : (t + 1) * depth, :]
        own = [jnp.where(lane_group == g, x, 0.0).astype(BF16) for g in range(group)]
        right = jnp.concatenate(own, axis=1)
        right = jnp.concatenate([right, right], axis=0)
        first = dot(left_in[...], right)
        time = embed[jnp.minimum(i, iters - 1) // ITERS]
        pre = first[:channels] + jnp.concatenate([time] * group, axis=1)
        hidden[t % 2] = (pre * jnp.tanh(pre) + pre).astype(BF16)
        direct[t % 4] = first[channels:]

    def mix(t):
        mixed = dot(mid_half[...], hidden[t % 2])
        second[t % 2] = (mixed * jnp.tanh(mixed) + mixed).astype(BF16)

    def leave(i, t, sums):
        r = i // ITERS
        at = slice(t * depth, (t + 1) * depth)
        x = state[at, :]
        noise = dot(left_out[...], second[t % 2]) + direct[t % 4]
        picked = noise[:, :window]
        for g in range(1, group):
            picked = jnp.where(lane_group == g, noise[:, g * window : (g + 1) * window], picked)
        drift = scales[r, 0:1] * x + scales[r, 1:2] * picked + bias[r]
        both = sum(dot(part, sums) for part in split3(drift))
        head = x[:, :1]
        change = both[:, :window] + head - x
        state[at, :] = both[:, window:] + head
        return change * change

    def sweep(i, carry):
        keep = (earlier < later).astype(F32).astype(BF16)
        moved = (earlier < limits[pl.ds(i, 1), :]).astype(F32).astype(BF16)
        sums = jnp.concatenate([keep, moved], axis=1)
        error = jnp.zeros((depth, window), F32)
        for t in range(tiles):
            enter(i + (t + 2) // tiles, (t + 2) % tiles)
            mix((t + 1) % tiles)
            error = error + leave(i, t, sums)
        squares[pl.ds(i, 1), :] = jnp.sum(error, axis=0, keepdims=True)
        return carry

    enter(0, 0)
    mix(0)
    enter(0, 1)
    lax.fori_loop(0, iters, sweep, 0)
    send_ref[pl.ds(0, window, stride=2), :] = state[...].T
    send_ref[pl.ds(1, window, stride=2), :] = squares[...].T


def finish(back_ref, final_ref, errors_ref):
    _, lat, pixels = final_ref.shape
    window = back_ref.shape[0] // 2
    rows = back_ref[pl.ds(0, window, stride=2), :].T
    for p in range(pixels // window):
        final_ref[0, :, p * window : (p + 1) * window] = rows[p * lat : (p + 1) * lat, :]
    totals = jnp.sum(back_ref[pl.ds(1, window, stride=2), :], axis=0, keepdims=True) * (1.0 / (lat * pixels))
    for r in range(ROUNDS):
        errors_ref[r] = totals[:, r * ITERS : (r + 1) * ITERS]


VMEM = pl.BlockSpec(memory_space=pltpu.VMEM)


def call(kernel, name, shapes, specs, scratch=(), limit=LIMIT):
    many = isinstance(shapes, (list, tuple))
    return pl.pallas_call(
        kernel,
        name=name,
        out_shape=shapes,
        in_specs=specs,
        out_specs=[VMEM] * len(shapes) if many else VMEM,
        scratch_shapes=list(scratch),
        compiler_params=pltpu.CompilerParams(vmem_limit_bytes=limit),
    )


def shape(dims, kind=F32):
    return jax.ShapeDtypeStruct(dims, kind)


def prep(advances, stamps, in_weight, time_weight, mid_weight, out_weight, group):
    channels, lat = in_weight.shape
    window = stamps.shape[1]
    depth = group * lat
    table_a, table_b = tables(channels)
    shapes = [
        shape((ROUNDS, channels, window)),
        shape((ROUNDS, depth, window)),
        shape((ROUNDS, 2, window)),
        shape((ROUNDS * ITERS, window), jnp.int32),
        shape((channels, channels), BF16),
        shape((channels + depth, 2 * depth), BF16),
        shape((depth, channels), BF16),
    ]
    specs = [pl.BlockSpec(memory_space=pltpu.SMEM)] + [VMEM] * 7
    return call(functools.partial(prepare, group), "prepare", shapes, specs)(
        advances, stamps, in_weight, time_weight, mid_weight, out_weight, jnp.asarray(table_a), jnp.asarray(table_b)
    )


def solve(received, ready, group):
    window, rows = received.shape
    channels = ready[4].shape[0]
    depth = ready[6].shape[0]
    scratch = [
        pltpu.VMEM((rows, window), F32),
        pltpu.VMEM((window, window), F32),
        pltpu.VMEM((2, channels, group * window), BF16),
        pltpu.VMEM((2, channels, group * window), BF16),
        pltpu.VMEM((4, depth, group * window), F32),
    ]
    kernel = functools.partial(picard, group)
    return call(kernel, "picard", shape((2 * window, rows)), [VMEM] * 8, scratch)(received, *ready)


def shards(states, t_sched, advances, in_weight, time_weight, mid_weight, out_weight):
    _, lat, pixels = states.shape
    window = lax.axis_size("steps")
    rows = lat * pixels // window
    start = jnp.stack([jnp.int32(0), advances[0]])
    stamps = jnp.stack(
        [lax.dynamic_slice_in_dim(t_sched, start[r] + n, window) for r in range(ROUNDS) for n in range(2)]
    )
    going = call(arrange, "arrange", shape((window, rows)), [VMEM])(states)
    received = lax.all_to_all(going, "steps", 0, 0, tiled=True)
    ready = prep(advances, stamps, in_weight, time_weight, mid_weight, out_weight, GROUP)
    send = solve(received, ready, GROUP)
    back = lax.all_to_all(send, "steps", 0, 0, tiled=True)
    final, errors = call(finish, "finish", [shape(states.shape), shape((ROUNDS, 1, ITERS))], [VMEM])(back)
    return final, errors.transpose(0, 2, 1)


def solution(mesh):
    both = ("groups", "steps")
    in_specs = (P(both, None, None), P("groups"), P("groups"), P(), P(), P(), P())
    out_specs = (P(both, None, None), P("groups", None, "steps"))
    return jax.shard_map(shards, mesh=mesh, in_specs=in_specs, out_specs=out_specs, check_vma=False)
```

time: 111 us -> 90.8 us (0.82)
  Pallas kernels: 46 us -> 29.8 us
  local copies, waits for them, and re-layouts: 7.37 us -> 3.69 us
  blocking collectives: 19.8 us -> 21.3 us
  waiting for transfers between devices: 8.7 us -> 7.22 us
    pallas_call x1 -> x4, Pallas kernels: 46 us -> 29.8 us  [the longest x1 26.4 us: solve(): call(kernel, 'picard', shape((2 * window, rows)), [VMEM] * 8, scratch)]
    all_to_all x3 -> x0, local copies, waits for them, and re-layouts: 2.7 us -> none  [the longest x1 1.57 us: shards(): received = lax.all_to_all(out_going, 'steps', 0, 0, tiled=True)]
    all_to_all x1, blocking collectives: 19.8 us -> 21.3 us  [shards(): back = lax.all_to_all(send, 'steps', 0, 0, tiled=True)]
    all_to_all x1, waiting for transfers between devices: 8.7 us -> 7.22 us  [shards(): received = lax.all_to_all(going, 'steps', 0, 0, tiled=True)]
    unnamed x9 -> x19, local copies, waits for them, and re-layouts: 3.3 us -> 3.61 us
  transfers between devices with their start and end apart: 1 -> 1, of which waited for: 1 -> 1; matrix products, arithmetic and copies ran while one was open for 1% -> 0% of each run, Pallas kernels for 0% -> 2%
where the time goes in v2:
time: 90.8 us; the launch traced here: 90.5 us
  Pallas kernels  29.8 us (33%)
  starting transfers between devices  27.5 us (30%)
  blocking collectives  21.3 us (23%)
  waiting for transfers between devices  7.22 us (8%)
  local copies, waits for them, and re-layouts  3.69 us (4%)
    all_to_all x1, starting transfers between devices, shards(): received = lax.all_to_all(going, 'steps', 0, 0, tiled=True)  27.5 us
    pallas_call x1, Pallas kernels, solve(): call(kernel, 'picard', shape((2 * window, rows)), [VMEM] * 8, scratch)  26.4 us
    all_to_all x1, blocking collectives, shards(): back = lax.all_to_all(send, 'steps', 0, 0, tiled=True)  21.3 us
    all_to_all x1, waiting for transfers between devices, shards(): received = lax.all_to_all(going, 'steps', 0, 0, tiled=True)  7.22 us
    unnamed x19, local copies, waits for them, and re-layouts  3.61 us
    pallas_call x1, Pallas kernels, prep(): call(functools.partial(prepare, group), 'prepare', shapes, specs)  1.98 us
  transfers between devices with their start and end apart: 1, of which 1 were waited for; matrix products, arithmetic and copies ran while one was open for 0% of the time, Pallas kernels for 2%

profile of v2, /device:TPU:513, one launch (start us, length us, event | category | flops | bytes accessed | tf_op | source)
XLA Modules:
  0.0 90.5 jit_solution(17657942216636152701)
XLA Ops:
  0.6 0.0 copy-start.1
  0.6 0.0 copy-start.4
  0.7 0.9 copy-done.4
  1.5 0.0 copy-start.6
  1.5 0.0 copy-start.8
  1.5 0.0 copy-start.7
  1.5 0.7 arrange.1
  2.3 0.0 copy-start.2
  2.3 27.5 %all-to-all-start = ((f32[128,1,128]{2,1,0:T(1,128)}), f32[128,1,128]{2,1,0:T(1,128)S(1)}, u32[]{:S(2)}, u32[]{:S(2)}) async-start(f32[128,1,128]{2,1,0:T(1,128)} %bitcast.1), calls=%async_computation | async-start | bytes 131072 | tf_op jit(solution)/shard_map/all_to_all | solution.py:301
  29.8 0.0 copy-done.6
  30.0 0.0 copy-done.8
  30.0 0.1 slice_bitcast_fusion.1
  30.1 0.0 copy-done.7
  30.1 0.2 copy.14.in_ref
  30.2 0.0 copy-start.5
  30.3 0.0 copy-done.1
  30.3 0.0 copy-done.2
  30.3 0.6 copy-done.5
  30.9 0.0 copy-start
  30.9 1.0 %copy-done = f32[320,320]{1,0:T(8,128)S(1)} copy-done((f32[320,320]{1,0:T(8,128)S(1)}, f32[320,320]{1,0:T(8,128)}, u32[]{:S(2)}) %copy-start) | copy-done | bytes 409624
  32.0 0.0 copy-start.3
  32.0 0.9 copy-done.3
  32.9 2.0 %prepare.1 = (f32[2,320,128]{2,1,0:T(8,128)S(1)}, f32[2,16,128]{2,1,0:T(8,128)S(1)}, f32[2,2,128]{2,1,0:T(2,128)S(1)}, s32[8,128]{1,0:T(8,128)S(1)}, bf16[320,32...) custom-call(s32[2]{0:T(128)S(1)} %copy-done.6, s32[4,128]{1,0:T(4,128)S(1)} %pad_add_fusion.stamps_ref, ...), custom_call_target="tpu_custom_call" | custom-call | tf_op jit(solution)/shard_map/prepare/pallas_call | solution.py:272
  34.8 7.2 %all-to-all-done = f32[128,1,128]{2,1,0:T(1,128)S(1)} async-done(((f32[128,1,128]{2,1,0:T(1,128)}), f32[128,1,128]{2,1,0:T(1,128)S(1)}, u32[]{:S(2)}, u32[]{:S(2)}) %all-to-all-start) | async-done | bytes 65568 | tf_op jit(solution)/shard_map/all_to_all | solution.py:301
  42.1 26.4 %picard.1 = f32[256,128]{1,0:T(8,128)S(1)} custom-call(f32[128,128]{1,0:T(8,128)S(1)} %bitcast.21, f32[2,320,128]{2,1,0:T(8,128)S(1)} %get-tuple-element.11.embed, f32[2,16,128]{2,1,0:T(8,128)S(1)} %get-tuple-element.12.bias, f32[2,2,128]{2,1,0:T(2,128)S(1)} %get-tuple-element.13.scales, s32[8,128]{1,0:T(8,128)S(1)} %get-tuple-element.14.limits, ...), custom_call_target="tpu_custom_call" | custom-call | tf_op jit(solution)/shard_map/picard/pallas_call | solution.py:289
  68.4 21.3 %all_to_all.22 = f32[128,2,128]{2,1,0:T(2,128)S(1)} all-to-all(f32[128,2,128]{2,1,0:T(2,128)S(1)} %bitcast.19), channel_id=1, replica_groups=mesh['groups'=2,'steps'=128] {'steps'}, dimensions={0} | all-to-all | bytes 262144 | tf_op jit(solution)/shard_map/all_to_all | solution.py:304
  89.8 0.7 finish.1
  (1 shorter events, 0.0 us)
Async XLA Ops:
  0.6 29.6 %copy-start.1 = (bf16[320,320]{1,0:T(8,128)(2,1)S(1)}, bf16[320,320]{1,0:T(8,128)(2,1)}, u32[]{:S(2)}) copy-start(bf16[320,320]{1,0:T(8,128)(2,1)} %mid_ref.1) | copy-start | bytes 614404
  0.6 0.9 copy-start.4
  1.5 28.3 %copy-start.6 = (s32[2]{0:T(128)S(1)}, s32[2]{0:T(128)}, u32[]{:S(2)}) copy-start(s32[2]{0:T(128)} %adv_ref.1) | copy-start | bytes 28
  1.5 28.5 %copy-start.8 = (s32[257]{0:T(512)S(1)}, s32[257]{0:T(512)}, u32[]{:S(2)}) copy-start(s32[257]{0:T(512)} %param.10) | copy-start | bytes 3088
  1.5 28.6 %copy-start.7 = (bf16[320,4]{0,1:T(4,128)(2,1)S(1)}, bf16[320,4]{0,1:T(4,128)(2,1)}, u32[]{:S(2)}) copy-start(bf16[320,4]{0,1:T(4,128)(2,1)} %param.12) | copy-start | bytes 7684
  2.3 28.0 %copy-start.2 = (bf16[384,96]{1,0:T(8,128)(2,1)S(1)}, bf16[384,96]{1,0:T(8,128)(2,1)}, u32[]{:S(2)}) copy-start(bf16[384,96]{1,0:T(8,128)(2,1)} %constant.12.clone.table_a_ref) | copy-start | bytes 221188
  2.3 39.8 %all-to-all-start = ((f32[128,1,128]{2,1,0:T(1,128)}), f32[128,1,128]{2,1,0:T(1,128)S(1)}, u32[]{:S(2)}, u32[]{:S(2)}) async-start(f32[128,1,128]{2,1,0:T(1,128)} %bitcast.1), calls=%async_computation | async-start | bytes 131072 | tf_op jit(solution)/shard_map/all_to_all | solution.py:301
  30.2 0.7 copy-start.5
  30.9 1.0 %copy-start = (f32[320,320]{1,0:T(8,128)S(1)}, f32[320,320]{1,0:T(8,128)}, u32[]{:S(2)}) copy-start(f32[320,320]{1,0:T(8,128)} %time_ref.1) | copy-start | bytes 1228804
  32.0 0.9 copy-start.3

commit v3 on v2

--- a/solution.py
+++ b/solution.py
@@ -159,6 +159,8 @@
     hidden,
     second,
     direct,
+    noise,
+    open_error,
 ):
     window, rows = recv_ref.shape
     channels = mid_half.shape[0]
@@ -188,37 +190,53 @@
         mixed = dot(mid_half[...], hidden[t % 2])
         second[t % 2] = (mixed * jnp.tanh(mixed) + mixed).astype(BF16)
 
-    def leave(i, t, sums):
+    def leave(t):
+        noise[t % 2] = dot(left_out[...], second[t % 2]) + direct[t % 4]
+
+    def advance(i, t, sums, live):
         r = i // ITERS
         at = slice(t * depth, (t + 1) * depth)
         x = state[at, :]
-        noise = dot(left_out[...], second[t % 2]) + direct[t % 4]
-        picked = noise[:, :window]
+        picked = noise[t % 2, :, :window]
         for g in range(1, group):
-            picked = jnp.where(lane_group == g, noise[:, g * window : (g + 1) * window], picked)
+            picked = jnp.where(lane_group == g, noise[t % 2, :, g * window : (g + 1) * window], picked)
         drift = scales[r, 0:1] * x + scales[r, 1:2] * picked + bias[r]
         both = sum(dot(part, sums) for part in split3(drift))
         head = x[:, :1]
         change = both[:, :window] + head - x
-        state[at, :] = both[:, window:] + head
+        after = both[:, window:] + head
+        state[at, :] = after if live is None else jnp.where(live, after, x)
         return change * change
 
-    def sweep(i, carry):
+    def sums_of(i):
         keep = (earlier < later).astype(F32).astype(BF16)
         moved = (earlier < limits[pl.ds(i, 1), :]).astype(F32).astype(BF16)
-        sums = jnp.concatenate([keep, moved], axis=1)
+        return jnp.concatenate([keep, moved], axis=1)
+
+    def close(i, error):
+        squares[pl.ds(i, 1), :] = jnp.sum(error, axis=0, keepdims=True)
+
+    def sweep(i, carry):
         error = jnp.zeros((depth, window), F32)
         for t in range(tiles):
             enter(i + (t + 2) // tiles, (t + 2) % tiles)
             mix((t + 1) % tiles)
-            error = error + leave(i, t, sums)
-        squares[pl.ds(i, 1), :] = jnp.sum(error, axis=0, keepdims=True)
+            if t == 0:
+                old = jnp.maximum(i - 1, 0)
+                close(old, open_error[...] + advance(old, tiles - 1, sums_of(old), i > 0))
+                sums = sums_of(i)
+            else:
+                error = error + advance(i, t - 1, sums, None)
+            leave(t)
+        open_error[...] = error
         return carry
 
     enter(0, 0)
     mix(0)
     enter(0, 1)
     lax.fori_loop(0, iters, sweep, 0)
+    last = iters - 1
+    close(last, open_error[...] + advance(last, tiles - 1, sums_of(last), None))
     send_ref[pl.ds(0, window, stride=2), :] = state[...].T
     send_ref[pl.ds(1, window, stride=2), :] = squares[...].T
 
@@ -284,6 +302,8 @@
         pltpu.VMEM((2, channels, group * window), BF16),
         pltpu.VMEM((2, channels, group * window), BF16),
         pltpu.VMEM((4, depth, group * window), F32),
+        pltpu.VMEM((2, depth, group * window), F32),
+        pltpu.VMEM((depth, window), F32),
     ]
     kernel = functools.partial(picard, group)
     return call(kernel, "picard", shape((2 * window, rows)), [VMEM] * 8, scratch)(received, *ready)

time: 90.8 us -> 86.7 us (0.955)
  Pallas kernels: 29.8 us -> 25.6 us
    pallas_call x1, Pallas kernels: 26.4 us -> 22.2 us  [solve(): call(kernel, 'picard', shape((2 * window, rows)), [VMEM] * 8, scratch)]
where the time goes in v3:
time: 86.7 us; the launch traced here: 86.3 us
  starting transfers between devices  27.5 us (32%)
  Pallas kernels  25.6 us (30%)
  blocking collectives  21.3 us (25%)
  waiting for transfers between devices  7.22 us (8%)
  local copies, waits for them, and re-layouts  3.69 us (4%)
  between operations  0.89 us (1%)
    all_to_all x1, starting transfers between devices, shards(): received = lax.all_to_all(going, 'steps', 0, 0, tiled=True)  27.5 us
    pallas_call x1, Pallas kernels, solve(): call(kernel, 'picard', shape((2 * window, rows)), [VMEM] * 8, scratch)  22.2 us
    all_to_all x1, blocking collectives, shards(): back = lax.all_to_all(send, 'steps', 0, 0, tiled=True)  21.3 us
    all_to_all x1, waiting for transfers between devices, shards(): received = lax.all_to_all(going, 'steps', 0, 0, tiled=True)  7.22 us
    unnamed x19, local copies, waits for them, and re-layouts  3.61 us
    pallas_call x1, Pallas kernels, prep(): call(functools.partial(prepare, group), 'prepare', shapes, specs)  1.98 us
  transfers between devices with their start and end apart: 1, of which 1 were waited for; matrix products, arithmetic and copies ran while one was open for 0% of the time, Pallas kernels for 2%

profile of v3, /device:TPU:513, one launch (start us, length us, event | category | flops | bytes accessed | tf_op | source)
XLA Modules:
  0.0 86.3 jit_solution(16949379684553449112)
XLA Ops:
  0.6 0.0 copy-start.1
  0.6 0.0 copy-start.4
  0.7 0.9 %copy-done.4 = f32[1,4,4096]{2,1,0:T(4,128)S(1)} copy-done((f32[1,4,4096]{2,1,0:T(4,128)S(1)}, f32[1,4,4096]{2,1,0:T(4,128)}, u32[]{:S(2)}) %copy-start.4) | copy-done | bytes 65560
  1.5 0.0 copy-start.6
  1.5 0.0 copy-start.8
  1.5 0.0 copy-start.7
  1.5 0.7 arrange.1
  2.3 0.0 copy-start.2
  2.3 27.5 %all-to-all-start = ((f32[128,1,128]{2,1,0:T(1,128)}), f32[128,1,128]{2,1,0:T(1,128)S(1)}, u32[]{:S(2)}, u32[]{:S(2)}) async-start(f32[128,1,128]{2,1,0:T(1,128)} %bitcast.1), calls=%async_computation | async-start | bytes 131072 | tf_op jit(solution)/shard_map/all_to_all | solution.py:321
  29.8 0.0 copy-done.6
  30.0 0.0 copy-done.8
  30.0 0.1 slice_bitcast_fusion.1
  30.1 0.0 copy-done.7
  30.1 0.2 copy.14.in_ref
  30.2 0.0 copy-start.5
  30.3 0.0 copy-done.1
  30.3 0.0 copy-done.2
  30.3 0.6 copy-done.5
  30.9 0.0 copy-start
  30.9 1.0 %copy-done = f32[320,320]{1,0:T(8,128)S(1)} copy-done((f32[320,320]{1,0:T(8,128)S(1)}, f32[320,320]{1,0:T(8,128)}, u32[]{:S(2)}) %copy-start) | copy-done | bytes 409624
  32.0 0.0 copy-start.3
  32.0 0.9 %copy-done.3 = bf16[320,96]{1,0:T(8,128)(2,1)S(1)} copy-done((bf16[320,96]{1,0:T(8,128)(2,1)S(1)}, bf16[320,96]{1,0:T(8,128)(2,1)}, u32[]{:S(2)}) %copy-start.3) | copy-done | bytes 61464
  32.9 2.0 %prepare.1 = (f32[2,320,128]{2,1,0:T(8,128)S(1)}, f32[2,16,128]{2,1,0:T(8,128)S(1)}, f32[2,2,128]{2,1,0:T(2,128)S(1)}, s32[8,128]{1,0:T(8,128)S(1)}, bf16[320,32...) custom-call(s32[2]{0:T(128)S(1)} %copy-done.6, s32[4,128]{1,0:T(4,128)S(1)} %pad_add_fusion.stamps_ref, ...), custom_call_target="tpu_custom_call" | custom-call | tf_op jit(solution)/shard_map/prepare/pallas_call | solution.py:290
  34.8 7.2 %all-to-all-done = f32[128,1,128]{2,1,0:T(1,128)S(1)} async-done(((f32[128,1,128]{2,1,0:T(1,128)}), f32[128,1,128]{2,1,0:T(1,128)S(1)}, u32[]{:S(2)}, u32[]{:S(2)}) %all-to-all-start) | async-done | bytes 65568 | tf_op jit(solution)/shard_map/all_to_all | solution.py:321
  42.1 22.2 %picard.1 = f32[256,128]{1,0:T(8,128)S(1)} custom-call(f32[128,128]{1,0:T(8,128)S(1)} %bitcast.21, f32[2,320,128]{2,1,0:T(8,128)S(1)} %get-tuple-element.11.embed, f32[2,16,128]{2,1,0:T(8,128)S(1)} %get-tuple-element.12.bias, f32[2,2,128]{2,1,0:T(2,128)S(1)} %get-tuple-element.13.scales, s32[8,128]{1,0:T(8,128)S(1)} %get-tuple-element.14.limits, ...), custom_call_target="tpu_custom_call" | custom-call | tf_op jit(solution)/shard_map/picard/pallas_call | solution.py:309
  64.2 21.3 %all_to_all.22 = f32[128,2,128]{2,1,0:T(2,128)S(1)} all-to-all(f32[128,2,128]{2,1,0:T(2,128)S(1)} %bitcast.19), channel_id=1, replica_groups=mesh['groups'=2,'steps'=128] {'steps'}, dimensions={0} | all-to-all | bytes 262144 | tf_op jit(solution)/shard_map/all_to_all | solution.py:324
  85.6 0.7 finish.1
  (1 shorter events, 0.0 us)
Async XLA Ops:
  0.6 29.6 %copy-start.1 = (bf16[320,320]{1,0:T(8,128)(2,1)S(1)}, bf16[320,320]{1,0:T(8,128)(2,1)}, u32[]{:S(2)}) copy-start(bf16[320,320]{1,0:T(8,128)(2,1)} %mid_ref.1) | copy-start | bytes 614404
  0.6 0.9 %copy-start.4 = (f32[1,4,4096]{2,1,0:T(4,128)S(1)}, f32[1,4,4096]{2,1,0:T(4,128)}, u32[]{:S(2)}) copy-start(f32[1,4,4096]{2,1,0:T(4,128)} %states_ref.1) | copy-start | bytes 196612
  1.5 28.3 %copy-start.6 = (s32[2]{0:T(128)S(1)}, s32[2]{0:T(128)}, u32[]{:S(2)}) copy-start(s32[2]{0:T(128)} %adv_ref.1) | copy-start | bytes 28
  1.5 28.5 %copy-start.8 = (s32[257]{0:T(512)S(1)}, s32[257]{0:T(512)}, u32[]{:S(2)}) copy-start(s32[257]{0:T(512)} %param.10) | copy-start | bytes 3088
  1.5 28.6 %copy-start.7 = (bf16[320,4]{0,1:T(4,128)(2,1)S(1)}, bf16[320,4]{0,1:T(4,128)(2,1)}, u32[]{:S(2)}) copy-start(bf16[320,4]{0,1:T(4,128)(2,1)} %param.12) | copy-start | bytes 7684
  2.3 28.0 %copy-start.2 = (bf16[384,96]{1,0:T(8,128)(2,1)S(1)}, bf16[384,96]{1,0:T(8,128)(2,1)}, u32[]{:S(2)}) copy-start(bf16[384,96]{1,0:T(8,128)(2,1)} %constant.12.clone.table_a_ref) | copy-start | bytes 221188
  2.3 39.8 %all-to-all-start = ((f32[128,1,128]{2,1,0:T(1,128)}), f32[128,1,128]{2,1,0:T(1,128)S(1)}, u32[]{:S(2)}, u32[]{:S(2)}) async-start(f32[128,1,128]{2,1,0:T(1,128)} %bitcast.1), calls=%async_computation | async-start | bytes 131072 | tf_op jit(solution)/shard_map/all_to_all | solution.py:321
  30.2 0.7 copy-start.5
  30.9 1.0 %copy-start = (f32[320,320]{1,0:T(8,128)S(1)}, f32[320,320]{1,0:T(8,128)}, u32[]{:S(2)}) copy-start(f32[320,320]{1,0:T(8,128)} %time_ref.1) | copy-start | bytes 1228804
  32.0 0.9 %copy-start.3 = (bf16[320,96]{1,0:T(8,128)(2,1)S(1)}, bf16[320,96]{1,0:T(8,128)(2,1)}, u32[]{:S(2)}) copy-start(bf16[320,96]{1,0:T(8,128)(2,1)} %constant.13.clone.table_b_ref) | copy-start | bytes 184324

commit v4 on v3

--- a/solution.py
+++ b/solution.py
@@ -8,6 +8,7 @@
 from jax import lax
 from jax.experimental import pallas as pl
 from jax.experimental.pallas import tpu as pltpu
+from jax.sharding import Mesh
 from jax.sharding import PartitionSpec as P
 
 TSTEPS = 1000
@@ -67,11 +68,24 @@
     return (lax.broadcasted_iota(jnp.int32, (count, row.shape[1]), 0) == row).astype(F32)
 
 
-def arrange(states_ref, going_ref):
+def in_pairs(even, odd):
+    own = lax.axis_index("cores") == 0
+    return jnp.where(own, even, odd), jnp.where(own, odd, even)
+
+
+def arrange(states_ref, keep_ref, give_ref, turned):
     _, lat, pixels = states_ref.shape
-    window = going_ref.shape[0]
+    window = turned.shape[0]
     blocks = [states_ref[0, :, p * window : (p + 1) * window] for p in range(pixels // window)]
-    going_ref[...] = jnp.concatenate(blocks, axis=0).T
+    turned[...] = jnp.concatenate(blocks, axis=0).T
+    half = pl.ds(0, window // 2, stride=2), pl.ds(1, window // 2, stride=2)
+    keep_ref[...], give_ref[...] = in_pairs(turned[half[0], :], turned[half[1], :])
+
+
+def merge(keep_ref, got_ref, both_ref):
+    count = keep_ref.shape[0]
+    both_ref[pl.ds(0, count, stride=2), :] = keep_ref[...]
+    both_ref[pl.ds(1, count, stride=2), :] = got_ref[...]
 
 
 def prepare(
@@ -122,12 +136,12 @@
     in_w = dot(in_ref[...], spread.astype(F32).astype(BF16))
     through = dot(out_w, in_w.astype(BF16))
     in_half = (in_w * 0.5).astype(BF16)
-    left_in[:channels, :depth] = in_half
-    left_in[:channels, depth:] = jnp.zeros_like(in_half)
+    left_in[:, :depth] = in_half
+    left_in[:, depth:] = jnp.zeros_like(in_half)
     high, low = split2(through)
-    left_in[channels:, :depth] = high
-    left_in[channels:, depth:] = low
-    left_out[...] = out_w
+    left_out[:, :channels] = out_w
+    left_out[:, channels : channels + depth] = high
+    left_out[:, channels + depth :] = low
     mid_half[...] = (mid_ref[...].astype(F32) * 0.5).astype(BF16)
     parts = split3(temb)
     bias_all = dot(out_w, parts[0]) + dot(out_w, parts[1]) + dot(out_w, parts[2])
@@ -153,12 +167,12 @@
     mid_half,
     left_in,
     left_out,
-    send_ref,
+    keep_ref,
+    give_ref,
     state,
     squares,
     hidden,
     second,
-    direct,
     noise,
     open_error,
 ):
@@ -169,7 +183,9 @@
     tiles = rows // depth
     iters = ROUNDS * ITERS
 
-    state[...] = recv_ref[...].T
+    half = pl.ds(0, window // 2, stride=2), pl.ds(1, window // 2, stride=2)
+    squares[half[0], :], squares[half[1], :] = in_pairs(recv_ref[half[0], :], recv_ref[half[1], :])
+    state[...] = squares[...].T
     squares[...] = jnp.zeros_like(squares)
     earlier = lax.broadcasted_iota(jnp.int32, (window, window), 0)
     later = lax.broadcasted_iota(jnp.int32, (window, window), 1)
@@ -181,27 +197,27 @@
         right = jnp.concatenate(own, axis=1)
         right = jnp.concatenate([right, right], axis=0)
         first = dot(left_in[...], right)
-        time = embed[jnp.minimum(i, iters - 1) // ITERS]
-        pre = first[:channels] + jnp.concatenate([time] * group, axis=1)
-        hidden[t % 2] = (pre * jnp.tanh(pre) + pre).astype(BF16)
-        direct[t % 4] = first[channels:]
+        pre = first + jnp.concatenate([embed[i // ITERS]] * group, axis=1)
+        hidden[t % 4, :channels] = (pre * jnp.tanh(pre) + pre).astype(BF16)
+        second[t % 4, channels:] = right
 
     def mix(t):
-        mixed = dot(mid_half[...], hidden[t % 2])
-        second[t % 2] = (mixed * jnp.tanh(mixed) + mixed).astype(BF16)
+        mixed = dot(mid_half[...], hidden[t % 4])
+        second[t % 4, :channels] = (mixed * jnp.tanh(mixed) + mixed).astype(BF16)
 
     def leave(t):
-        noise[t % 2] = dot(left_out[...], second[t % 2]) + direct[t % 4]
+        noise[t % 4] = dot(left_out[...], second[t % 4])
 
     def advance(i, t, sums, live):
         r = i // ITERS
         at = slice(t * depth, (t + 1) * depth)
         x = state[at, :]
-        picked = noise[t % 2, :, :window]
+        picked = noise[t % 4, :, :window]
         for g in range(1, group):
-            picked = jnp.where(lane_group == g, noise[t % 2, :, g * window : (g + 1) * window], picked)
+            picked = jnp.where(lane_group == g, noise[t % 4, :, g * window : (g + 1) * window], picked)
         drift = scales[r, 0:1] * x + scales[r, 1:2] * picked + bias[r]
-        both = sum(dot(part, sums) for part in split3(drift))
+        wide = dot(jnp.concatenate(split3(drift), axis=0), sums)
+        both = wide[:depth] + wide[depth : 2 * depth] + wide[2 * depth :]
         head = x[:, :1]
         change = both[:, :window] + head - x
         after = both[:, window:] + head
@@ -216,38 +232,62 @@
     def close(i, error):
         squares[pl.ds(i, 1), :] = jnp.sum(error, axis=0, keepdims=True)
 
-    def sweep(i, carry):
-        error = jnp.zeros((depth, window), F32)
+    def sweep(i, carry, last=False):
+        fixed = isinstance(i, int)
+        old = max(i - 1, 0) if fixed else jnp.maximum(i - 1, 0)
+        sums = sums_of(old)
+        error = open_error[...]
         for t in range(tiles):
-            enter(i + (t + 2) // tiles, (t + 2) % tiles)
-            mix((t + 1) % tiles)
-            if t == 0:
-                old = jnp.maximum(i - 1, 0)
-                close(old, open_error[...] + advance(old, tiles - 1, sums_of(old), i > 0))
+            if t == 2:
+                close(old, error)
                 sums = sums_of(i)
+                error = jnp.zeros((depth, window), F32)
+            if t < 2:
+                error = error + advance(old, tiles + t - 2, sums, None if fixed else i > 0)
             else:
-                error = error + advance(i, t - 1, sums, None)
+                error = error + advance(i, t - 2, sums, None)
+            if not last or t + 2 < tiles:
+                enter(i + (t + 2) // tiles, (t + 2) % tiles)
+            if not last or t + 1 < tiles:
+                mix((t + 1) % tiles)
             leave(t)
         open_error[...] = error
         return carry
 
-    enter(0, 0)
-    mix(0)
-    enter(0, 1)
-    lax.fori_loop(0, iters, sweep, 0)
-    last = iters - 1
-    close(last, open_error[...] + advance(last, tiles - 1, sums_of(last), None))
-    send_ref[pl.ds(0, window, stride=2), :] = state[...].T
-    send_ref[pl.ds(1, window, stride=2), :] = squares[...].T
-
-
-def finish(back_ref, final_ref, errors_ref):
+    final = iters - 1
+    for t in range(2):
+        enter(0, t)
+        if t < 1:
+            mix(t)
+
+    def several(j, carry):
+        for u in range(3):
+            sweep(j * 3 + u, carry)
+        return carry
+
+    whole = final // 3
+    lax.fori_loop(0, whole, several, 0)
+    for u in range(whole * 3, final):
+        sweep(u, 0)
+    sweep(final, 0, True)
+    error = open_error[...]
+    for t in range(tiles - 2, tiles):
+        error = error + advance(final, t, sums_of(final), None)
+    close(final, error)
+    for kind, ref in enumerate((state, squares)):
+        ref[...] = ref[...].T
+        keep_ref[half[kind], :], give_ref[half[kind], :] = in_pairs(ref[half[0], :], ref[half[1], :])
+
+
+def finish(back_ref, final_ref, errors_ref, rows):
     _, lat, pixels = final_ref.shape
-    window = back_ref.shape[0] // 2
-    rows = back_ref[pl.ds(0, window, stride=2), :].T
+    window = rows.shape[0]
+    parts = [back_ref[pl.ds(k, window // 2, stride=4), :] for k in range(4)]
+    rows[pl.ds(0, window // 2, stride=2), :], rows[pl.ds(1, window // 2, stride=2), :] = in_pairs(parts[0], parts[2])
+    turned = rows[...].T
     for p in range(pixels // window):
-        final_ref[0, :, p * window : (p + 1) * window] = rows[p * lat : (p + 1) * lat, :]
-    totals = jnp.sum(back_ref[pl.ds(1, window, stride=2), :], axis=0, keepdims=True) * (1.0 / (lat * pixels))
+        final_ref[0, :, p * window : (p + 1) * window] = turned[p * lat : (p + 1) * lat, :]
+    totals = jnp.sum(parts[1] + parts[3], axis=0, keepdims=True) * (1.0 / (lat * pixels))
     for r in range(ROUNDS):
         errors_ref[r] = totals[:, r * ITERS : (r + 1) * ITERS]
 
@@ -283,8 +323,8 @@
         shape((ROUNDS, 2, window)),
         shape((ROUNDS * ITERS, window), jnp.int32),
         shape((channels, channels), BF16),
-        shape((channels + depth, 2 * depth), BF16),
-        shape((depth, channels), BF16),
+        shape((channels, 2 * depth), BF16),
+        shape((depth, channels + 2 * depth), BF16),
     ]
     specs = [pl.BlockSpec(memory_space=pltpu.SMEM)] + [VMEM] * 7
     return call(functools.partial(prepare, group), "prepare", shapes, specs)(
@@ -299,35 +339,49 @@
     scratch = [
         pltpu.VMEM((rows, window), F32),
         pltpu.VMEM((window, window), F32),
-        pltpu.VMEM((2, channels, group * window), BF16),
-        pltpu.VMEM((2, channels, group * window), BF16),
+        pltpu.VMEM((4, channels, group * window), BF16),
+        pltpu.VMEM((4, channels + 2 * depth, group * window), BF16),
         pltpu.VMEM((4, depth, group * window), F32),
-        pltpu.VMEM((2, depth, group * window), F32),
         pltpu.VMEM((depth, window), F32),
     ]
     kernel = functools.partial(picard, group)
-    return call(kernel, "picard", shape((2 * window, rows)), [VMEM] * 8, scratch)(received, *ready)
+    return call(kernel, "picard", [shape((window, rows))] * 2, [VMEM] * 8, scratch)(received, *ready)
+
+
+def swap(give):
+    return lax.ppermute(give, "cores", [(0, 1), (1, 0)])
+
+
+def to_chips(rows):
+    chips = lax.axis_size("chips")
+    return lax.all_to_all(rows.reshape(chips, -1, rows.shape[-1]), "chips", 0, 0, tiled=True).reshape(-1, rows.shape[-1])
 
 
 def shards(states, t_sched, advances, in_weight, time_weight, mid_weight, out_weight):
     _, lat, pixels = states.shape
-    window = lax.axis_size("steps")
+    window = lax.axis_size(("chips", "cores"))
     rows = lat * pixels // window
     start = jnp.stack([jnp.int32(0), advances[0]])
     stamps = jnp.stack(
         [lax.dynamic_slice_in_dim(t_sched, start[r] + n, window) for r in range(ROUNDS) for n in range(2)]
     )
-    going = call(arrange, "arrange", shape((window, rows)), [VMEM])(states)
-    received = lax.all_to_all(going, "steps", 0, 0, tiled=True)
+    halves = [shape((window // 2, rows))] * 2
+    keep, give = call(arrange, "arrange", halves, [VMEM], [pltpu.VMEM((window, rows), F32)])(states)
+    received = to_chips(call(merge, "merge", shape((window, rows)), [VMEM] * 2)(keep, swap(give)))
     ready = prep(advances, stamps, in_weight, time_weight, mid_weight, out_weight, GROUP)
-    send = solve(received, ready, GROUP)
-    back = lax.all_to_all(send, "steps", 0, 0, tiled=True)
-    final, errors = call(finish, "finish", [shape(states.shape), shape((ROUNDS, 1, ITERS))], [VMEM])(back)
+    keep, give = solve(received, ready, GROUP)
+    chips = lax.axis_size("chips")
+    pair = [part.reshape(chips, -1, rows) for part in (keep, swap(give))]
+    back = to_chips(jnp.concatenate(pair, axis=1).reshape(-1, rows))
+    outs = [shape(states.shape), shape((ROUNDS, 1, ITERS))]
+    final, errors = call(finish, "finish", outs, [VMEM], [pltpu.VMEM((window, rows), F32)])(back)
     return final, errors.transpose(0, 2, 1)
 
 
 def solution(mesh):
-    both = ("groups", "steps")
-    in_specs = (P(both, None, None), P("groups"), P("groups"), P(), P(), P(), P())
-    out_specs = (P(both, None, None), P("groups", None, "steps"))
-    return jax.shard_map(shards, mesh=mesh, in_specs=in_specs, out_specs=out_specs, check_vma=False)
+    groups, steps = mesh.shape["groups"], mesh.shape["steps"]
+    split = Mesh(mesh.devices.reshape(groups, steps // 2, 2), ("groups", "chips", "cores"))
+    every = ("groups", "chips", "cores")
+    in_specs = (P(every, None, None), P("groups"), P("groups"), P(), P(), P(), P())
+    out_specs = (P(every, None, None), P("groups", None, every[1:]))
+    return jax.shard_map(shards, mesh=split, in_specs=in_specs, out_specs=out_specs, check_vma=False)

time: 86.7 us -> 82.3 us (0.949)
  blocking collectives: 21.3 us -> 16.2 us
  between operations: 0.89 us -> 3.98 us
  Pallas kernels: 25.6 us -> 23.4 us
  starting transfers between devices: 27.5 us -> 28.6 us
  local copies, waits for them, and re-layouts: 3.69 us -> 2.81 us
    ppermute x0 -> x2, starting transfers between devices: none -> 22 us  [swap(): return lax.ppermute(give, 'cores', [(0, 1), (1, 0)])]
    all_to_all x1, starting transfers between devices: 27.5 us -> 6.61 us  [to_chips(): lax.all_to_all(rows.reshape(chips, -1, rows.shape[-1]), 'chips', 0, 0, ti...]
    all_to_all x1, blocking collectives: 21.3 us -> 16.2 us  [to_chips(): lax.all_to_all(rows.reshape(chips, -1, rows.shape[-1]), 'chips', 0, 0, ti...]
    pallas_call x3 -> x4, Pallas kernels: 23.6 us -> 21.5 us  [the longest x1 20 us: solve(): call(kernel, 'picard', [shape((window, rows))] * 2, [VMEM] * 8, scratch)]
    all_to_all x1, waiting for transfers between devices: 7.22 us -> 5.94 us  [to_chips(): lax.all_to_all(rows.reshape(chips, -1, rows.shape[-1]), 'chips', 0, 0, ti...]
    ppermute x0 -> x2, waiting for transfers between devices: none -> 0.9 us  [swap(): return lax.ppermute(give, 'cores', [(0, 1), (1, 0)])]
    unnamed x19, local copies, waits for them, and re-layouts: 3.61 us -> 2.73 us
  transfers between devices with their start and end apart: 1 -> 3, of which waited for: 1 -> 2; matrix products, arithmetic and copies ran while one was open for 0% -> 0% of each run, Pallas kernels for 2% -> 2%
where the time goes in v4:
time: 82.3 us; the launch traced here: 81.9 us
  starting transfers between devices  28.6 us (35%)
  Pallas kernels  23.4 us (28%)
  blocking collectives  16.2 us (20%)
  waiting for transfers between devices  6.85 us (8%)
  between operations  3.98 us (5%)
  local copies, waits for them, and re-layouts  2.81 us (3%)
    ppermute x2, starting transfers between devices, swap(): return lax.ppermute(give, 'cores', [(0, 1), (1, 0)])  22 us
    pallas_call x1, Pallas kernels, solve(): call(kernel, 'picard', [shape((window, rows))] * 2, [VMEM] * 8, scratch)  20 us
    all_to_all x1, blocking collectives, to_chips(): lax.all_to_all(rows.reshape(chips, -1, rows.shape[-1]), 'chips', 0, 0, ti...  16.2 us
    all_to_all x1, starting transfers between devices, to_chips(): lax.all_to_all(rows.reshape(chips, -1, rows.shape[-1]), 'chips', 0, 0, ti...  6.61 us
    all_to_all x1, waiting for transfers between devices, to_chips(): lax.all_to_all(rows.reshape(chips, -1, rows.shape[-1]), 'chips', 0, 0, ti...  5.94 us
    unnamed x19, local copies, waits for them, and re-layouts  2.73 us
    pallas_call x1, Pallas kernels, prep(): call(functools.partial(prepare, group), 'prepare', shapes, specs)  1.97 us
  transfers between devices with their start and end apart: 3, of which 2 were waited for; matrix products, arithmetic and copies ran while one was open for 0% of the time, Pallas kernels for 2%

profile of v4, /device:TPU:513, one launch (start us, length us, event | category | flops | bytes accessed | tf_op | source)
XLA Modules:
  0.0 81.9 jit_solution(16360204748595514960)
XLA Ops:
  0.6 0.0 copy-start.1
  0.6 0.0 copy-start.4
  0.6 0.9 %copy-done.4 = f32[1,4,4096]{2,1,0:T(4,128)S(1)} copy-done((f32[1,4,4096]{2,1,0:T(4,128)S(1)}, f32[1,4,4096]{2,1,0:T(4,128)}, u32[]{:S(2)}) %copy-start.4) | copy-done | bytes 65560
  1.5 0.1 arrange.1
  1.6 20.5 %collective-permute-start = (f32[64,128]{1,0:T(8,128)S(1)}, f32[64,128]{1,0:T(8,128)S(1)}, u32[]{:S(2)}, u32[]{:S(2)}) collective-permute-start(f32[64,128]{1,0:T(8,128)S(1)} %get-tuple-element.16), channel_id=1, source_target_pairs={{0,1},{1,0},{2,3},{3,2},{4,5},{5,4},{6,7},{7,6},{8,9},{9,8},{10,11... | collective-permute-start | bytes 98312 | tf_op jit(solution)/shard_map/ppermute | solution.py:352
  25.4 0.0 collective-permute-done.got_ref
  25.4 0.6 merge.1
  26.1 0.0 copy-start.8
  26.1 0.0 copy-start.7
  26.1 0.0 copy-start.2
  26.1 6.6 %all-to-all-start = ((f32[64,2,128]{2,1,0:T(2,128)}), f32[64,2,128]{2,1,0:T(2,128)S(1)}, u32[]{:S(2)}, u32[]{:S(2)}) async-start(f32[64,2,128]{2,1,0:T(2,128)} %bitcast), calls=%async_computation | async-start | bytes 131072 | tf_op jit(solution)/shard_map/all_to_all | solution.py:357
  32.7 0.0 copy-done.8
  32.7 0.0 copy-start.3
  32.7 0.1 slice_bitcast_fusion.1
  32.8 0.0 copy-done.7
  32.8 0.2 copy.11.in_ref
  32.9 0.0 copy-start.5
  32.9 0.0 copy-start.6
  33.0 0.0 copy-done.1
  33.0 0.0 copy-done.2
  33.0 0.6 copy-done.3
  33.6 0.1 copy-done.5
  33.6 0.0 copy-done.6
  33.6 0.0 copy-start
  33.6 1.0 %copy-done = f32[320,320]{1,0:T(8,128)S(1)} copy-done((f32[320,320]{1,0:T(8,128)S(1)}, f32[320,320]{1,0:T(8,128)}, u32[]{:S(2)}) %copy-start) | copy-done | bytes 409624
  34.7 2.0 %prepare.1 = (f32[2,320,128]{2,1,0:T(8,128)S(1)}, f32[2,16,128]{2,1,0:T(8,128)S(1)}, f32[2,2,128]{2,1,0:T(2,128)S(1)}, s32[8,128]{1,0:T(8,128)S(1)}, bf16[320,32...) custom-call(s32[2]{0:T(128)S(1)} %copy-done.6, s32[4,128]{1,0:T(4,128)S(1)} %pad_add_fusion.stamps_ref, ...), custom_call_target="tpu_custom_call" | custom-call | tf_op jit(solution)/shard_map/prepare/pallas_call | solution.py:330
  36.6 5.9 %all-to-all-done = f32[64,2,128]{2,1,0:T(2,128)S(1)} async-done(((f32[64,2,128]{2,1,0:T(2,128)}), f32[64,2,128]{2,1,0:T(2,128)S(1)}, u32[]{:S(2)}, u32[]{:S(2)}) %all-to-all-start) | async-done | bytes 65568 | tf_op jit(solution)/shard_map/all_to_all | solution.py:357
  42.6 20.0 %picard.1 = (f32[128,128]{1,0:T(8,128)S(1)}, f32[128,128]{1,0:T(8,128)S(1)}) custom-call(f32[128,128]{1,0:T(8,128)S(1)} %bitcast.19, f32[2,320,128]{2,1,0:T(8,128)S(1)} %get-tuple-element.17.embed, f32[2,16,128]{2,1,0:T(8,128)S(1)} %get-tuple-element.18.bias, f32[2,2,128]{2,1,0:T(2,128)S(1)} %get-tuple-element.19.scales, ...), custom_call_target="tpu_custom_call" | custom-call | tf_op jit(solution)/shard_map/picard/pallas_call | solution.py:348
  62.6 1.4 %collective-permute-start.1 = (f32[128,128]{1,0:T(8,128)S(1)}, f32[128,128]{1,0:T(8,128)S(1)}, u32[]{:S(2)}, u32[]{:S(2)}) collective-permute-start(f32[128,128]{1,0:T(8,128)S(1)} %get-tuple-element.25), channel_id=1, source_target_pairs={{0,1},{1,0},{2,3},{3,2},{4,5},{5,4},{6,7},{7,6},{8,9},{9,8},{10,11... | collective-permute-start | bytes 196616 | tf_op jit(solution)/shard_map/ppermute | solution.py:352
  64.0 0.9 %collective-permute-done.1 = f32[128,128]{1,0:T(8,128)S(1)} collective-permute-done((f32[128,128]{1,0:T(8,128)S(1)}, f32[128,128]{1,0:T(8,128)S(1)}, u32[]{:S(2)}, u32[]{:S(2)}) %collective-permute-start.1) | collective-permute-done | bytes 65568 | tf_op jit(solution)/shard_map/ppermute | solution.py:352
  64.9 0.1 pad_maximum_fusion
  65.0 16.2 %all_to_all.10 = f32[64,4,128]{2,1,0:T(4,128)S(1)} all-to-all(f32[64,4,128]{2,1,0:T(4,128)S(1)} %pad_maximum_fusion), channel_id=1, replica_groups=mesh['groups'=2,'chips'=64,'cores'=2] {'chips'}, dimensions={0} | all-to-all | bytes 262144 | tf_op jit(solution)/shard_map/all_to_all | solution.py:357
  81.2 0.7 finish.1
  (1 shorter events, 0.0 us)
Async XLA Ops:
  0.6 32.4 %copy-start.1 = (bf16[320,320]{1,0:T(8,128)(2,1)S(1)}, bf16[320,320]{1,0:T(8,128)(2,1)}, u32[]{:S(2)}) copy-start(bf16[320,320]{1,0:T(8,128)(2,1)} %mid_ref.1) | copy-start | bytes 614404
  0.6 0.9 %copy-start.4 = (f32[1,4,4096]{2,1,0:T(4,128)S(1)}, f32[1,4,4096]{2,1,0:T(4,128)}, u32[]{:S(2)}) copy-start(f32[1,4,4096]{2,1,0:T(4,128)} %states_ref.1) | copy-start | bytes 196612
  1.6 23.8 %collective-permute-start = (f32[64,128]{1,0:T(8,128)S(1)}, f32[64,128]{1,0:T(8,128)S(1)}, u32[]{:S(2)}, u32[]{:S(2)}) collective-permute-start(f32[64,128]{1,0:T(8,128)S(1)} %get-tuple-element.16), channel_id=1, source_target_pairs={{0,1},{1,0},{2,3},{3,2},{4,5},{5,4},{6,7},{7,6},{8,9},{9,8},{10,11... | collective-permute-start | bytes 98312 | tf_op jit(solution)/shard_map/ppermute | solution.py:352
  26.1 6.6 %copy-start.8 = (s32[257]{0:T(512)S(1)}, s32[257]{0:T(512)}, u32[]{:S(2)}) copy-start(s32[257]{0:T(512)} %param.10) | copy-start | bytes 3088
  26.1 6.7 %copy-start.7 = (bf16[320,4]{0,1:T(4,128)(2,1)S(1)}, bf16[320,4]{0,1:T(4,128)(2,1)}, u32[]{:S(2)}) copy-start(bf16[320,4]{0,1:T(4,128)(2,1)} %param.12) | copy-start | bytes 7684
  26.1 6.9 %copy-start.2 = (bf16[384,96]{1,0:T(8,128)(2,1)S(1)}, bf16[384,96]{1,0:T(8,128)(2,1)}, u32[]{:S(2)}) copy-start(bf16[384,96]{1,0:T(8,128)(2,1)} %constant.12.clone.table_a_ref) | copy-start | bytes 221188
  26.1 16.5 %all-to-all-start = ((f32[64,2,128]{2,1,0:T(2,128)}), f32[64,2,128]{2,1,0:T(2,128)S(1)}, u32[]{:S(2)}, u32[]{:S(2)}) async-start(f32[64,2,128]{2,1,0:T(2,128)} %bitcast), calls=%async_computation | async-start | bytes 131072 | tf_op jit(solution)/shard_map/all_to_all | solution.py:357
  32.7 0.9 %copy-start.3 = (bf16[320,96]{1,0:T(8,128)(2,1)S(1)}, bf16[320,96]{1,0:T(8,128)(2,1)}, u32[]{:S(2)}) copy-start(bf16[320,96]{1,0:T(8,128)(2,1)} %constant.13.clone.table_b_ref) | copy-start | bytes 184324
  32.9 0.7 copy-start.5
  32.9 0.7 copy-start.6
  33.6 1.0 %copy-start = (f32[320,320]{1,0:T(8,128)S(1)}, f32[320,320]{1,0:T(8,128)}, u32[]{:S(2)}) copy-start(f32[320,320]{1,0:T(8,128)} %time_ref.1) | copy-start | bytes 1228804
  62.6 2.3 %collective-permute-start.1 = (f32[128,128]{1,0:T(8,128)S(1)}, f32[128,128]{1,0:T(8,128)S(1)}, u32[]{:S(2)}, u32[]{:S(2)}) collective-permute-start(f32[128,128]{1,0:T(8,128)S(1)} %get-tuple-element.25), channel_id=1, source_target_pairs={{0,1},{1,0},{2,3},{3,2},{4,5},{5,4},{6,7},{7,6},{8,9},{9,8},{10,11... | collective-permute-start | bytes 196616 | tf_op jit(solution)/shard_map/ppermute | solution.py:352

commit v5 on v4

--- a/solution.py
+++ b/solution.py
@@ -16,6 +16,7 @@
 ROUNDS = 2
 RADIX = 32
 GROUP = 4
+LANES = 128
 LIMIT = 16 * 1024 * 1024
 F32 = jnp.float32
 BF16 = jnp.bfloat16
@@ -91,7 +92,7 @@
 def prepare(
     group,
     adv_ref,
-    stamps_ref,
+    sched_ref,
     in_ref,
     time_ref,
     mid_ref,
@@ -105,14 +106,19 @@
     mid_half,
     left_in,
     left_out,
+    padded,
 ):
-    window = stamps_ref.shape[1]
+    window = embed.shape[2]
     channels, lat = in_ref.shape
     half = channels // 2
     depth = group * lat
 
-    stamps = stamps_ref[...]
-    row = jnp.concatenate([stamps[k : k + 1] for k in (0, 2, 1, 3)], axis=1)
+    length = sched_ref.shape[1]
+    padded[0:1, :length] = sched_ref[...]
+    plan = padded[...]
+    starts = [0, adv_ref[0]]
+    rolled = [pltpu.roll(plan, padded.shape[1] - start - n, 1) if r or n else plan for n in range(2) for r, start in enumerate(starts)]
+    row = jnp.concatenate([stamps[:1, :window] for stamps in rolled], axis=1)
     hot_a = one_hot(row // RADIX, RADIX).astype(BF16)
     hot_b = one_hot(row % RADIX, RADIX)
     hot_a3 = jnp.concatenate([hot_a] * 3, axis=0)
@@ -312,9 +318,9 @@
     return jax.ShapeDtypeStruct(dims, kind)
 
 
-def prep(advances, stamps, in_weight, time_weight, mid_weight, out_weight, group):
+def prep(advances, t_sched, in_weight, time_weight, mid_weight, out_weight, group, window):
     channels, lat = in_weight.shape
-    window = stamps.shape[1]
+    lanes = -(-t_sched.shape[0] // LANES) * LANES
     depth = group * lat
     table_a, table_b = tables(channels)
     shapes = [
@@ -327,8 +333,8 @@
         shape((depth, channels + 2 * depth), BF16),
     ]
     specs = [pl.BlockSpec(memory_space=pltpu.SMEM)] + [VMEM] * 7
-    return call(functools.partial(prepare, group), "prepare", shapes, specs)(
-        advances, stamps, in_weight, time_weight, mid_weight, out_weight, jnp.asarray(table_a), jnp.asarray(table_b)
+    return call(functools.partial(prepare, group), "prepare", shapes, specs, [pltpu.VMEM((8, lanes), jnp.int32)])(
+        advances, t_sched.reshape(1, -1), in_weight, time_weight, mid_weight, out_weight, jnp.asarray(table_a), jnp.asarray(table_b)
     )
 
 
@@ -361,14 +367,10 @@
     _, lat, pixels = states.shape
     window = lax.axis_size(("chips", "cores"))
     rows = lat * pixels // window
-    start = jnp.stack([jnp.int32(0), advances[0]])
-    stamps = jnp.stack(
-        [lax.dynamic_slice_in_dim(t_sched, start[r] + n, window) for r in range(ROUNDS) for n in range(2)]
-    )
     halves = [shape((window // 2, rows))] * 2
     keep, give = call(arrange, "arrange", halves, [VMEM], [pltpu.VMEM((window, rows), F32)])(states)
     received = to_chips(call(merge, "merge", shape((window, rows)), [VMEM] * 2)(keep, swap(give)))
-    ready = prep(advances, stamps, in_weight, time_weight, mid_weight, out_weight, GROUP)
+    ready = prep(advances, t_sched, in_weight, time_weight, mid_weight, out_weight, GROUP, window)
     keep, give = solve(received, ready, GROUP)
     chips = lax.axis_size("chips")
     pair = [part.reshape(chips, -1, rows) for part in (keep, swap(give))]

time: 82.3 us -> 80.9 us (0.983)
  between operations: 3.98 us -> 0.73 us
    ppermute x2, waiting for transfers between devices: 0.9 us -> 1.76 us  [swap(): return lax.ppermute(give, 'cores', [(0, 1), (1, 0)])]
    all_to_all x1, blocking collectives: 16.2 us -> 17 us  [to_chips(): lax.all_to_all(rows.reshape(chips, -1, rows.shape[-1]), 'chips', 0, 0, ti...]
  transfers between devices with their start and end apart: 3 -> 3, of which waited for: 2 -> 3; matrix products, arithmetic and copies ran while one was open for 0% -> 0% of each run, Pallas kernels for 2% -> 3%
where the time goes in v5:
time: 80.9 us; the launch traced here: 80.5 us
  starting transfers between devices  28.8 us (36%)
  Pallas kernels  23.5 us (29%)
  blocking collectives  17 us (21%)
  waiting for transfers between devices  6.96 us (9%)
  local copies, waits for them, and re-layouts  3.46 us (4%)
    ppermute x2, starting transfers between devices, swap(): return lax.ppermute(give, 'cores', [(0, 1), (1, 0)])  22.2 us
    pallas_call x1, Pallas kernels, solve(): call(kernel, 'picard', [shape((window, rows))] * 2, [VMEM] * 8, scratch)  20 us
    all_to_all x1, blocking collectives, to_chips(): lax.all_to_all(rows.reshape(chips, -1, rows.shape[-1]), 'chips', 0, 0, ti...  17 us
    all_to_all x1, starting transfers between devices, to_chips(): lax.all_to_all(rows.reshape(chips, -1, rows.shape[-1]), 'chips', 0, 0, ti...  6.61 us
    all_to_all x1, waiting for transfers between devices, to_chips(): lax.all_to_all(rows.reshape(chips, -1, rows.shape[-1]), 'chips', 0, 0, ti...  5.2 us
    unnamed x19, local copies, waits for them, and re-layouts  3.46 us
    pallas_call x1, Pallas kernels, prep(): call(functools.partial(prepare, group), 'prepare', shapes, specs, [pltpu....  2.05 us
    ppermute x2, waiting for transfers between devices, swap(): return lax.ppermute(give, 'cores', [(0, 1), (1, 0)])  1.76 us
  transfers between devices with their start and end apart: 3, of which 3 were waited for; matrix products, arithmetic and copies ran while one was open for 0% of the time, Pallas kernels for 3%

profile of v5, /device:TPU:513, one launch (start us, length us, event | category | flops | bytes accessed | tf_op | source)
XLA Modules:
  0.0 80.5 jit_solution(10503595205068256955)
XLA Ops:
  0.6 0.0 copy-start.1
  0.6 0.0 copy-start.4
  0.6 0.9 %copy-done.4 = f32[1,4,4096]{2,1,0:T(4,128)S(1)} copy-done((f32[1,4,4096]{2,1,0:T(4,128)S(1)}, f32[1,4,4096]{2,1,0:T(4,128)}, u32[]{:S(2)}) %copy-start.4) | copy-done | bytes 65560
  1.5 0.1 arrange.1
  1.6 20.5 %collective-permute-start = (f32[64,128]{1,0:T(8,128)S(1)}, f32[64,128]{1,0:T(8,128)S(1)}, u32[]{:S(2)}, u32[]{:S(2)}) collective-permute-start(f32[64,128]{1,0:T(8,128)S(1)} %get-tuple-element.16), channel_id=1, source_target_pairs={{0,1},{1,0},{2,3},{3,2},{4,5},{5,4},{6,7},{7,6},{8,9},{9,8},{10,11... | collective-permute-start | bytes 98312 | tf_op jit(solution)/shard_map/ppermute | solution.py:358
  22.2 0.9 %collective-permute-done.got_ref = f32[64,128]{1,0:T(8,128)S(1)} collective-permute-done((f32[64,128]{1,0:T(8,128)S(1)}, f32[64,128]{1,0:T(8,128)S(1)}, u32[]{:S(2)}, u32[]{:S(2)}) %collective-permute-start) | collective-permute-done | bytes 32800 | tf_op jit(solution)/shard_map/ppermute | solution.py:358
  23.0 0.0 copy-start.8
  23.0 0.0 copy-start.7
  23.0 0.6 merge.1
  23.7 0.0 copy-start.2
  23.7 6.6 %all-to-all-start = ((f32[64,2,128]{2,1,0:T(2,128)}), f32[64,2,128]{2,1,0:T(2,128)S(1)}, u32[]{:S(2)}, u32[]{:S(2)}) async-start(f32[64,2,128]{2,1,0:T(2,128)} %bitcast), calls=%async_computation | async-start | bytes 131072 | tf_op jit(solution)/shard_map/all_to_all | solution.py:363
  30.3 0.0 copy-done.8
  30.3 0.0 copy-done.7
  30.3 0.0 copy-start.5
  30.3 0.0 copy-start.6
  30.3 0.2 copy.11.in_ref
  30.5 0.0 copy-done.1
  30.5 0.0 copy-done.2
  30.5 0.5 copy-done.5
  31.0 0.0 copy-done.6
  31.0 0.0 copy-start
  31.0 1.0 %copy-done = f32[320,320]{1,0:T(8,128)S(1)} copy-done((f32[320,320]{1,0:T(8,128)S(1)}, f32[320,320]{1,0:T(8,128)}, u32[]{:S(2)}) %copy-start) | copy-done | bytes 409624
  32.0 0.0 copy-start.3
  32.0 0.9 %copy-done.3 = bf16[320,96]{1,0:T(8,128)(2,1)S(1)} copy-done((bf16[320,96]{1,0:T(8,128)(2,1)S(1)}, bf16[320,96]{1,0:T(8,128)(2,1)}, u32[]{:S(2)}) %copy-start.3) | copy-done | bytes 61464
  32.9 2.1 %prepare.1 = (f32[2,320,128]{2,1,0:T(8,128)S(1)}, f32[2,16,128]{2,1,0:T(8,128)S(1)}, f32[2,2,128]{2,1,0:T(2,128)S(1)}, s32[8,128]{1,0:T(8,128)S(1)}, bf16[320,32...) custom-call(s32[2]{0:T(128)S(1)} %copy-done.6, s32[1,257]{1,0:T(1,128)S(1)} %reshape.24.sched_ref, ...), custom_call_target="tpu_custom_call" | custom-call | tf_op jit(solution)/shard_map/prepare/pallas_call | solution.py:336
  35.0 5.2 %all-to-all-done = f32[64,2,128]{2,1,0:T(2,128)S(1)} async-done(((f32[64,2,128]{2,1,0:T(2,128)}), f32[64,2,128]{2,1,0:T(2,128)S(1)}, u32[]{:S(2)}, u32[]{:S(2)}) %all-to-all-start) | async-done | bytes 65568 | tf_op jit(solution)/shard_map/all_to_all | solution.py:363
  40.2 20.0 %picard.1 = (f32[128,128]{1,0:T(8,128)S(1)}, f32[128,128]{1,0:T(8,128)S(1)}) custom-call(f32[128,128]{1,0:T(8,128)S(1)} %bitcast.9, f32[2,320,128]{2,1,0:T(8,128)S(1)} %get-tuple-element.17.embed, f32[2,16,128]{2,1,0:T(8,128)S(1)} %get-tuple-element.18.bias, f32[2,2,128]{2,1,0:T(2,128)S(1)} %get-tuple-element.19.scales, ...), custom_call_target="tpu_custom_call" | custom-call | tf_op jit(solution)/shard_map/picard/pallas_call | solution.py:354
  60.2 1.6 %collective-permute-start.1 = (f32[128,128]{1,0:T(8,128)S(1)}, f32[128,128]{1,0:T(8,128)S(1)}, u32[]{:S(2)}, u32[]{:S(2)}) collective-permute-start(f32[128,128]{1,0:T(8,128)S(1)} %get-tuple-element.25), channel_id=1, source_target_pairs={{0,1},{1,0},{2,3},{3,2},{4,5},{5,4},{6,7},{7,6},{8,9},{9,8},{10,11... | collective-permute-start | bytes 196616 | tf_op jit(solution)/shard_map/ppermute | solution.py:358
  61.8 0.9 %collective-permute-done.1 = f32[128,128]{1,0:T(8,128)S(1)} collective-permute-done((f32[128,128]{1,0:T(8,128)S(1)}, f32[128,128]{1,0:T(8,128)S(1)}, u32[]{:S(2)}, u32[]{:S(2)}) %collective-permute-start.1) | collective-permute-done | bytes 65568 | tf_op jit(solution)/shard_map/ppermute | solution.py:358
  62.7 0.1 pad_maximum_fusion
  62.8 17.0 %all_to_all.10 = f32[64,4,128]{2,1,0:T(4,128)S(1)} all-to-all(f32[64,4,128]{2,1,0:T(4,128)S(1)} %pad_maximum_fusion), channel_id=1, replica_groups=mesh['groups'=2,'chips'=64,'cores'=2] {'chips'}, dimensions={0} | all-to-all | bytes 262144 | tf_op jit(solution)/shard_map/all_to_all | solution.py:363
  79.8 0.7 finish.1
  (1 shorter events, 0.0 us)
Async XLA Ops:
  0.6 29.9 %copy-start.1 = (bf16[320,320]{1,0:T(8,128)(2,1)S(1)}, bf16[320,320]{1,0:T(8,128)(2,1)}, u32[]{:S(2)}) copy-start(bf16[320,320]{1,0:T(8,128)(2,1)} %mid_ref.1) | copy-start | bytes 614404
  0.6 0.9 %copy-start.4 = (f32[1,4,4096]{2,1,0:T(4,128)S(1)}, f32[1,4,4096]{2,1,0:T(4,128)}, u32[]{:S(2)}) copy-start(f32[1,4,4096]{2,1,0:T(4,128)} %states_ref.1) | copy-start | bytes 196612
  1.6 21.4 %collective-permute-start = (f32[64,128]{1,0:T(8,128)S(1)}, f32[64,128]{1,0:T(8,128)S(1)}, u32[]{:S(2)}, u32[]{:S(2)}) collective-permute-start(f32[64,128]{1,0:T(8,128)S(1)} %get-tuple-element.16), channel_id=1, source_target_pairs={{0,1},{1,0},{2,3},{3,2},{4,5},{5,4},{6,7},{7,6},{8,9},{9,8},{10,11... | collective-permute-start | bytes 98312 | tf_op jit(solution)/shard_map/ppermute | solution.py:358
  23.0 7.3 %copy-start.8 = (s32[257]{0:T(512)S(1)}, s32[257]{0:T(512)}, u32[]{:S(2)}) copy-start(s32[257]{0:T(512)} %param.10) | copy-start | bytes 3088
  23.0 7.3 %copy-start.7 = (bf16[320,4]{0,1:T(4,128)(2,1)S(1)}, bf16[320,4]{0,1:T(4,128)(2,1)}, u32[]{:S(2)}) copy-start(bf16[320,4]{0,1:T(4,128)(2,1)} %param.12) | copy-start | bytes 7684
  23.7 6.8 %copy-start.2 = (bf16[384,96]{1,0:T(8,128)(2,1)S(1)}, bf16[384,96]{1,0:T(8,128)(2,1)}, u32[]{:S(2)}) copy-start(bf16[384,96]{1,0:T(8,128)(2,1)} %constant.4.clone.table_a_ref) | copy-start | bytes 221188
  23.7 16.5 %all-to-all-start = ((f32[64,2,128]{2,1,0:T(2,128)}), f32[64,2,128]{2,1,0:T(2,128)S(1)}, u32[]{:S(2)}, u32[]{:S(2)}) async-start(f32[64,2,128]{2,1,0:T(2,128)} %bitcast), calls=%async_computation | async-start | bytes 131072 | tf_op jit(solution)/shard_map/all_to_all | solution.py:363
  30.3 0.7 copy-start.5
  30.3 0.7 copy-start.6
  31.0 1.0 %copy-start = (f32[320,320]{1,0:T(8,128)S(1)}, f32[320,320]{1,0:T(8,128)}, u32[]{:S(2)}) copy-start(f32[320,320]{1,0:T(8,128)} %time_ref.1) | copy-start | bytes 1228804
  32.0 0.9 %copy-start.3 = (bf16[320,96]{1,0:T(8,128)(2,1)S(1)}, bf16[320,96]{1,0:T(8,128)(2,1)}, u32[]{:S(2)}) copy-start(bf16[320,96]{1,0:T(8,128)(2,1)} %constant.5.clone.table_b_ref) | copy-start | bytes 184324
  60.2 2.5 %collective-permute-start.1 = (f32[128,128]{1,0:T(8,128)S(1)}, f32[128,128]{1,0:T(8,128)S(1)}, u32[]{:S(2)}, u32[]{:S(2)}) collective-permute-start(f32[128,128]{1,0:T(8,128)S(1)} %get-tuple-element.25), channel_id=1, source_target_pairs={{0,1},{1,0},{2,3},{3,2},{4,5},{5,4},{6,7},{7,6},{8,9},{9,8},{10,11... | collective-permute-start | bytes 196616 | tf_op jit(solution)/shard_map/ppermute | solution.py:358

commit v6 on v5

--- a/solution.py
+++ b/solution.py
@@ -16,6 +16,7 @@
 ROUNDS = 2
 RADIX = 32
 GROUP = 4
+BY_HAND = 64
 LANES = 128
 LIMIT = 16 * 1024 * 1024
 F32 = jnp.float32
@@ -87,6 +88,16 @@
     count = keep_ref.shape[0]
     both_ref[pl.ds(0, count, stride=2), :] = keep_ref[...]
     both_ref[pl.ds(1, count, stride=2), :] = got_ref[...]
+
+
+def cut(blocks, whole):
+    for b in range(blocks.shape[0]):
+        width = min(LANES, whole.shape[1] - b * LANES)
+        blocks[b, :, :width] = whole[:, b * LANES : b * LANES + width]
+
+
+def joined(blocks, width):
+    return jnp.concatenate([blocks[b, :, : min(LANES, width - b * LANES)] for b in range(blocks.shape[0])], axis=1)
 
 
 def prepare(
@@ -106,6 +117,7 @@
     mid_half,
     left_in,
     left_out,
+    spread_in,
     padded,
 ):
     window = embed.shape[2]
@@ -145,10 +157,10 @@
     left_in[:, :depth] = in_half
     left_in[:, depth:] = jnp.zeros_like(in_half)
     high, low = split2(through)
-    left_out[:, :channels] = out_w
-    left_out[:, channels : channels + depth] = high
-    left_out[:, channels + depth :] = low
-    mid_half[...] = (mid_ref[...].astype(F32) * 0.5).astype(BF16)
+    cut(left_out, jnp.concatenate([out_w, jnp.concatenate([high, low], axis=1)], axis=1))
+    for c in range(lat):
+        spread_in[c] = jnp.broadcast_to(in_half[channels - BY_HAND :, c : c + 1].astype(F32), (BY_HAND, window))
+    cut(mid_half, (mid_ref[...].astype(F32) * 0.5).astype(BF16))
     parts = split3(temb)
     bias_all = dot(out_w, parts[0]) + dot(out_w, parts[1]) + dot(out_w, parts[2])
     place = lax.broadcasted_iota(jnp.int32, (1, window), 1)
@@ -173,6 +185,7 @@
     mid_half,
     left_in,
     left_out,
+    spread_in,
     keep_ref,
     give_ref,
     state,
@@ -183,8 +196,8 @@
     open_error,
 ):
     window, rows = recv_ref.shape
-    channels = mid_half.shape[0]
-    depth = left_out.shape[0]
+    channels = mid_half.shape[1]
+    depth = left_out.shape[1]
     lat = depth // group
     tiles = rows // depth
     iters = ROUNDS * ITERS
@@ -202,17 +215,24 @@
         own = [jnp.where(lane_group == g, x, 0.0).astype(BF16) for g in range(group)]
         right = jnp.concatenate(own, axis=1)
         right = jnp.concatenate([right, right], axis=0)
-        first = dot(left_in[...], right)
-        pre = first + jnp.concatenate([embed[i // ITERS]] * group, axis=1)
-        hidden[t % 4, :channels] = (pre * jnp.tanh(pre) + pre).astype(BF16)
+        low = x.astype(BF16).astype(F32)
+        split = channels - BY_HAND
+        first = dot(left_in[:split], right)
+        pre = first + jnp.concatenate([embed[i // ITERS, :split]] * group, axis=1)
+        hidden[t % 4, :split] = (pre * jnp.tanh(pre) + pre).astype(BF16)
+        for g in range(group):
+            pre = embed[i // ITERS, split:]
+            for c in range(lat):
+                pre = pre + spread_in[c] * low[g * lat + c : g * lat + c + 1, :]
+            hidden[t % 4, split:, g * window : (g + 1) * window] = (pre * jnp.tanh(pre) + pre).astype(BF16)
         second[t % 4, channels:] = right
 
     def mix(t):
-        mixed = dot(mid_half[...], hidden[t % 4])
+        mixed = dot(joined(mid_half, channels), hidden[t % 4])
         second[t % 4, :channels] = (mixed * jnp.tanh(mixed) + mixed).astype(BF16)
 
     def leave(t):
-        noise[t % 4] = dot(left_out[...], second[t % 4])
+        noise[t % 4] = dot(joined(left_out, channels + 2 * depth), second[t % 4])
 
     def advance(i, t, sums, live):
         r = i // ITERS
@@ -252,8 +272,8 @@
                 error = error + advance(old, tiles + t - 2, sums, None if fixed else i > 0)
             else:
                 error = error + advance(i, t - 2, sums, None)
-            if not last or t + 2 < tiles:
-                enter(i + (t + 2) // tiles, (t + 2) % tiles)
+            if not last or t + 3 < tiles:
+                enter(i + (t + 3) // tiles, (t + 3) % tiles)
             if not last or t + 1 < tiles:
                 mix((t + 1) % tiles)
             leave(t)
@@ -261,7 +281,7 @@
         return carry
 
     final = iters - 1
-    for t in range(2):
+    for t in range(3):
         enter(0, t)
         if t < 1:
             mix(t)
@@ -328,9 +348,10 @@
         shape((ROUNDS, depth, window)),
         shape((ROUNDS, 2, window)),
         shape((ROUNDS * ITERS, window), jnp.int32),
-        shape((channels, channels), BF16),
+        shape((-(-channels // LANES), channels, LANES), BF16),
         shape((channels, 2 * depth), BF16),
-        shape((depth, channels + 2 * depth), BF16),
+        shape((-(-(channels + 2 * depth) // LANES), depth, LANES), BF16),
+        shape((lat, BY_HAND, window)),
     ]
     specs = [pl.BlockSpec(memory_space=pltpu.SMEM)] + [VMEM] * 7
     return call(functools.partial(prepare, group), "prepare", shapes, specs, [pltpu.VMEM((8, lanes), jnp.int32)])(
@@ -340,8 +361,8 @@
 
 def solve(received, ready, group):
     window, rows = received.shape
-    channels = ready[4].shape[0]
-    depth = ready[6].shape[0]
+    channels = ready[4].shape[1]
+    depth = ready[6].shape[1]
     scratch = [
         pltpu.VMEM((rows, window), F32),
         pltpu.VMEM((window, window), F32),
@@ -351,7 +372,7 @@
         pltpu.VMEM((depth, window), F32),
     ]
     kernel = functools.partial(picard, group)
-    return call(kernel, "picard", [shape((window, rows))] * 2, [VMEM] * 8, scratch)(received, *ready)
+    return call(kernel, "picard", [shape((window, rows))] * 2, [VMEM] * 9, scratch)(received, *ready)
 
 
 def swap(give):

time: 80.9 us -> 80 us (0.989)
    pallas_call x1, Pallas kernels: 20 us -> 19.1 us  [solve(): call(kernel, 'picard', [shape((window, rows))] * 2, [VMEM] * 9, scratch)]
where the time goes in v6:
time: 80 us; the launch traced here: 79.7 us
  starting transfers between devices  28.8 us (36%)
  Pallas kernels  22.7 us (28%)
  blocking collectives  17.1 us (21%)
  waiting for transfers between devices  6.93 us (9%)
  local copies, waits for them, and re-layouts  3.46 us (4%)
    ppermute x2, starting transfers between devices, swap(): return lax.ppermute(give, 'cores', [(0, 1), (1, 0)])  22.1 us
    pallas_call x1, Pallas kernels, solve(): call(kernel, 'picard', [shape((window, rows))] * 2, [VMEM] * 9, scratch)  19.1 us
    all_to_all x1, blocking collectives, to_chips(): lax.all_to_all(rows.reshape(chips, -1, rows.shape[-1]), 'chips', 0, 0, ti...  17.1 us
    all_to_all x1, starting transfers between devices, to_chips(): lax.all_to_all(rows.reshape(chips, -1, rows.shape[-1]), 'chips', 0, 0, ti...  6.61 us
    all_to_all x1, waiting for transfers between devices, to_chips(): lax.all_to_all(rows.reshape(chips, -1, rows.shape[-1]), 'chips', 0, 0, ti...  5.17 us
    unnamed x19, local copies, waits for them, and re-layouts  3.46 us
    pallas_call x1, Pallas kernels, prep(): call(functools.partial(prepare, group), 'prepare', shapes, specs, [pltpu....  2.08 us
    ppermute x2, waiting for transfers between devices, swap(): return lax.ppermute(give, 'cores', [(0, 1), (1, 0)])  1.76 us
  transfers between devices with their start and end apart: 3, of which 3 were waited for; matrix products, arithmetic and copies ran while one was open for 0% of the time, Pallas kernels for 3%

profile of v6, /device:TPU:513, one launch (start us, length us, event | category | flops | bytes accessed | tf_op | source)
XLA Modules:
  0.0 79.7 jit_solution(12437632078342583853)
XLA Ops:
  0.6 0.0 copy-start.1
  0.6 0.0 copy-start.4
  0.6 0.9 %copy-done.4 = f32[1,4,4096]{2,1,0:T(4,128)S(1)} copy-done((f32[1,4,4096]{2,1,0:T(4,128)S(1)}, f32[1,4,4096]{2,1,0:T(4,128)}, u32[]{:S(2)}) %copy-start.4) | copy-done | bytes 65560
  1.5 0.1 arrange.1
  1.6 20.5 %collective-permute-start = (f32[64,128]{1,0:T(8,128)S(1)}, f32[64,128]{1,0:T(8,128)S(1)}, u32[]{:S(2)}, u32[]{:S(2)}) collective-permute-start(f32[64,128]{1,0:T(8,128)S(1)} %get-tuple-element.17), channel_id=1, source_target_pairs={{0,1},{1,0},{2,3},{3,2},{4,5},{5,4},{6,7},{7,6},{8,9},{9,8},{10,11... | collective-permute-start | bytes 98312 | tf_op jit(solution)/shard_map/ppermute | solution.py:379
  22.2 0.9 %collective-permute-done.got_ref = f32[64,128]{1,0:T(8,128)S(1)} collective-permute-done((f32[64,128]{1,0:T(8,128)S(1)}, f32[64,128]{1,0:T(8,128)S(1)}, u32[]{:S(2)}, u32[]{:S(2)}) %collective-permute-start) | collective-permute-done | bytes 32800 | tf_op jit(solution)/shard_map/ppermute | solution.py:379
  23.0 0.0 copy-start.8
  23.0 0.0 copy-start.7
  23.0 0.6 merge.1
  23.7 0.0 copy-start.2
  23.7 6.6 %all-to-all-start = ((f32[64,2,128]{2,1,0:T(2,128)}), f32[64,2,128]{2,1,0:T(2,128)S(1)}, u32[]{:S(2)}, u32[]{:S(2)}) async-start(f32[64,2,128]{2,1,0:T(2,128)} %bitcast), calls=%async_computation | async-start | bytes 131072 | tf_op jit(solution)/shard_map/all_to_all | solution.py:384
  30.3 0.0 copy-done.8
  30.3 0.0 copy-done.7
  30.3 0.0 copy-start.5
  30.3 0.0 copy-start.6
  30.3 0.2 copy.11.in_ref
  30.5 0.0 copy-done.1
  30.5 0.0 copy-done.2
  30.5 0.5 copy-done.5
  31.0 0.0 copy-done.6
  31.0 0.0 copy-start
  31.0 1.0 %copy-done = f32[320,320]{1,0:T(8,128)S(1)} copy-done((f32[320,320]{1,0:T(8,128)S(1)}, f32[320,320]{1,0:T(8,128)}, u32[]{:S(2)}) %copy-start) | copy-done | bytes 409624
  32.0 0.0 copy-start.3
  32.0 0.9 %copy-done.3 = bf16[320,96]{1,0:T(8,128)(2,1)S(1)} copy-done((bf16[320,96]{1,0:T(8,128)(2,1)S(1)}, bf16[320,96]{1,0:T(8,128)(2,1)}, u32[]{:S(2)}) %copy-start.3) | copy-done | bytes 61464
  32.9 2.1 %prepare.1 = (f32[2,320,128]{2,1,0:T(8,128)S(1)}, f32[2,16,128]{2,1,0:T(8,128)S(1)}, f32[2,2,128]{2,1,0:T(2,128)S(1)}, s32[8,128]{1,0:T(8,128)S(1)}, bf16[3,320,...) custom-call(s32[2]{0:T(128)S(1)} %copy-done.6, ...), custom_call_target="tpu_custom_call" | custom-call | tf_op jit(solution)/shard_map/prepare/pallas_call | solution.py:357
  35.0 5.2 %all-to-all-done = f32[64,2,128]{2,1,0:T(2,128)S(1)} async-done(((f32[64,2,128]{2,1,0:T(2,128)}), f32[64,2,128]{2,1,0:T(2,128)S(1)}, u32[]{:S(2)}, u32[]{:S(2)}) %all-to-all-start) | async-done | bytes 65568 | tf_op jit(solution)/shard_map/all_to_all | solution.py:384
  40.2 19.1 %picard.1 = (f32[128,128]{1,0:T(8,128)S(1)}, f32[128,128]{1,0:T(8,128)S(1)}) custom-call(f32[128,128]{1,0:T(8,128)S(1)} %bitcast.9, f32[2,320,128]{2,1,0:T(8,128)S(1)} %get-tuple-element.18.embed, f32[2,16,128]{2,1,0:T(8,128)S(1)} %get-tuple-element.19.bias, f32[2,2,128]{2,1,0:T(2,128)S(1)} %get-tuple-element.20.scales, ...), custom_call_target="tpu_custom_call" | custom-call | tf_op jit(solution)/shard_map/picard/pallas_call | solution.py:375
  59.3 1.6 %collective-permute-start.1 = (f32[128,128]{1,0:T(8,128)S(1)}, f32[128,128]{1,0:T(8,128)S(1)}, u32[]{:S(2)}, u32[]{:S(2)}) collective-permute-start(f32[128,128]{1,0:T(8,128)S(1)} %get-tuple-element.27), channel_id=1, source_target_pairs={{0,1},{1,0},{2,3},{3,2},{4,5},{5,4},{6,7},{7,6},{8,9},{9,8},{10,11... | collective-permute-start | bytes 196616 | tf_op jit(solution)/shard_map/ppermute | solution.py:379
  60.9 0.9 %collective-permute-done.1 = f32[128,128]{1,0:T(8,128)S(1)} collective-permute-done((f32[128,128]{1,0:T(8,128)S(1)}, f32[128,128]{1,0:T(8,128)S(1)}, u32[]{:S(2)}, u32[]{:S(2)}) %collective-permute-start.1) | collective-permute-done | bytes 65568 | tf_op jit(solution)/shard_map/ppermute | solution.py:379
  61.8 0.1 pad_maximum_fusion
  61.9 17.1 %all_to_all.10 = f32[64,4,128]{2,1,0:T(4,128)S(1)} all-to-all(f32[64,4,128]{2,1,0:T(4,128)S(1)} %pad_maximum_fusion), channel_id=1, replica_groups=mesh['groups'=2,'chips'=64,'cores'=2] {'chips'}, dimensions={0} | all-to-all | bytes 262144 | tf_op jit(solution)/shard_map/all_to_all | solution.py:384
  79.0 0.7 finish.1
  (1 shorter events, 0.0 us)
Async XLA Ops:
  0.6 29.9 %copy-start.1 = (bf16[320,320]{1,0:T(8,128)(2,1)S(1)}, bf16[320,320]{1,0:T(8,128)(2,1)}, u32[]{:S(2)}) copy-start(bf16[320,320]{1,0:T(8,128)(2,1)} %mid_ref.1) | copy-start | bytes 614404
  0.6 0.9 %copy-start.4 = (f32[1,4,4096]{2,1,0:T(4,128)S(1)}, f32[1,4,4096]{2,1,0:T(4,128)}, u32[]{:S(2)}) copy-start(f32[1,4,4096]{2,1,0:T(4,128)} %states_ref.1) | copy-start | bytes 196612
  1.6 21.4 %collective-permute-start = (f32[64,128]{1,0:T(8,128)S(1)}, f32[64,128]{1,0:T(8,128)S(1)}, u32[]{:S(2)}, u32[]{:S(2)}) collective-permute-start(f32[64,128]{1,0:T(8,128)S(1)} %get-tuple-element.17), channel_id=1, source_target_pairs={{0,1},{1,0},{2,3},{3,2},{4,5},{5,4},{6,7},{7,6},{8,9},{9,8},{10,11... | collective-permute-start | bytes 98312 | tf_op jit(solution)/shard_map/ppermute | solution.py:379
  23.0 7.3 %copy-start.8 = (s32[257]{0:T(512)S(1)}, s32[257]{0:T(512)}, u32[]{:S(2)}) copy-start(s32[257]{0:T(512)} %param.10) | copy-start | bytes 3088
  23.0 7.3 %copy-start.7 = (bf16[320,4]{0,1:T(4,128)(2,1)S(1)}, bf16[320,4]{0,1:T(4,128)(2,1)}, u32[]{:S(2)}) copy-start(bf16[320,4]{0,1:T(4,128)(2,1)} %param.12) | copy-start | bytes 7684
  23.7 6.8 %copy-start.2 = (bf16[384,96]{1,0:T(8,128)(2,1)S(1)}, bf16[384,96]{1,0:T(8,128)(2,1)}, u32[]{:S(2)}) copy-start(bf16[384,96]{1,0:T(8,128)(2,1)} %constant.4.clone.table_a_ref) | copy-start | bytes 221188
  23.7 16.5 %all-to-all-start = ((f32[64,2,128]{2,1,0:T(2,128)}), f32[64,2,128]{2,1,0:T(2,128)S(1)}, u32[]{:S(2)}, u32[]{:S(2)}) async-start(f32[64,2,128]{2,1,0:T(2,128)} %bitcast), calls=%async_computation | async-start | bytes 131072 | tf_op jit(solution)/shard_map/all_to_all | solution.py:384
  30.3 0.7 copy-start.5
  30.3 0.7 copy-start.6
  31.0 1.0 %copy-start = (f32[320,320]{1,0:T(8,128)S(1)}, f32[320,320]{1,0:T(8,128)}, u32[]{:S(2)}) copy-start(f32[320,320]{1,0:T(8,128)} %time_ref.1) | copy-start | bytes 1228804
  32.0 0.9 %copy-start.3 = (bf16[320,96]{1,0:T(8,128)(2,1)S(1)}, bf16[320,96]{1,0:T(8,128)(2,1)}, u32[]{:S(2)}) copy-start(bf16[320,96]{1,0:T(8,128)(2,1)} %constant.5.clone.table_b_ref) | copy-start | bytes 184324
  59.3 2.5 %collective-permute-start.1 = (f32[128,128]{1,0:T(8,128)S(1)}, f32[128,128]{1,0:T(8,128)S(1)}, u32[]{:S(2)}, u32[]{:S(2)}) collective-permute-start(f32[128,128]{1,0:T(8,128)S(1)} %get-tuple-element.27), channel_id=1, source_target_pairs={{0,1},{1,0},{2,3},{3,2},{4,5},{5,4},{6,7},{7,6},{8,9},{9,8},{10,11... | collective-permute-start | bytes 196616 | tf_op jit(solution)/shard_map/ppermute | solution.py:379

commit v7 on v6

--- a/solution.py
+++ b/solution.py
@@ -242,8 +242,8 @@
         for g in range(1, group):
             picked = jnp.where(lane_group == g, noise[t % 4, :, g * window : (g + 1) * window], picked)
         drift = scales[r, 0:1] * x + scales[r, 1:2] * picked + bias[r]
-        wide = dot(jnp.concatenate(split3(drift), axis=0), sums)
-        both = wide[:depth] + wide[depth : 2 * depth] + wide[2 * depth :]
+        wide = dot(jnp.concatenate(split2(drift), axis=0), sums)
+        both = wide[:depth] + wide[depth:]
         head = x[:, :1]
         change = both[:, :window] + head - x
         after = both[:, window:] + head

time: 80 us -> 79.9 us (level)
  no operation moved by 1% of the time
where the time goes in v7:
time: 79.9 us; the launch traced here: 79.6 us
  starting transfers between devices  28.7 us (36%)
  Pallas kernels  22.6 us (28%)
  blocking collectives  17.1 us (21%)
  waiting for transfers between devices  6.93 us (9%)
  local copies, waits for them, and re-layouts  3.46 us (4%)
    ppermute x2, starting transfers between devices, swap(): return lax.ppermute(give, 'cores', [(0, 1), (1, 0)])  22.1 us
    pallas_call x1, Pallas kernels, solve(): call(kernel, 'picard', [shape((window, rows))] * 2, [VMEM] * 9, scratch)  19 us
    all_to_all x1, blocking collectives, to_chips(): lax.all_to_all(rows.reshape(chips, -1, rows.shape[-1]), 'chips', 0, 0, ti...  17.1 us
    all_to_all x1, starting transfers between devices, to_chips(): lax.all_to_all(rows.reshape(chips, -1, rows.shape[-1]), 'chips', 0, 0, ti...  6.61 us
    all_to_all x1, waiting for transfers between devices, to_chips(): lax.all_to_all(rows.reshape(chips, -1, rows.shape[-1]), 'chips', 0, 0, ti...  5.17 us
    unnamed x19, local copies, waits for them, and re-layouts  3.46 us
    pallas_call x1, Pallas kernels, prep(): call(functools.partial(prepare, group), 'prepare', shapes, specs, [pltpu....  2.08 us
    ppermute x2, waiting for transfers between devices, swap(): return lax.ppermute(give, 'cores', [(0, 1), (1, 0)])  1.76 us
  transfers between devices with their start and end apart: 3, of which 3 were waited for; matrix products, arithmetic and copies ran while one was open for 0% of the time, Pallas kernels for 3%

profile of v7, /device:TPU:513, one launch (start us, length us, event | category | flops | bytes accessed | tf_op | source)
XLA Modules:
  0.0 79.6 jit_solution(5834803730055346979)
XLA Ops:
  0.6 0.0 copy-start.1
  0.6 0.0 copy-start.4
  0.6 0.9 %copy-done.4 = f32[1,4,4096]{2,1,0:T(4,128)S(1)} copy-done((f32[1,4,4096]{2,1,0:T(4,128)S(1)}, f32[1,4,4096]{2,1,0:T(4,128)}, u32[]{:S(2)}) %copy-start.4) | copy-done | bytes 65560
  1.5 0.1 arrange.1
  1.6 20.5 %collective-permute-start = (f32[64,128]{1,0:T(8,128)S(1)}, f32[64,128]{1,0:T(8,128)S(1)}, u32[]{:S(2)}, u32[]{:S(2)}) collective-permute-start(f32[64,128]{1,0:T(8,128)S(1)} %get-tuple-element.17), channel_id=1, source_target_pairs={{0,1},{1,0},{2,3},{3,2},{4,5},{5,4},{6,7},{7,6},{8,9},{9,8},{10,11... | collective-permute-start | bytes 98312 | tf_op jit(solution)/shard_map/ppermute | solution.py:379
  22.2 0.9 %collective-permute-done.got_ref = f32[64,128]{1,0:T(8,128)S(1)} collective-permute-done((f32[64,128]{1,0:T(8,128)S(1)}, f32[64,128]{1,0:T(8,128)S(1)}, u32[]{:S(2)}, u32[]{:S(2)}) %collective-permute-start) | collective-permute-done | bytes 32800 | tf_op jit(solution)/shard_map/ppermute | solution.py:379
  23.0 0.0 copy-start.8
  23.0 0.0 copy-start.7
  23.0 0.6 merge.1
  23.7 0.0 copy-start.2
  23.7 6.6 %all-to-all-start = ((f32[64,2,128]{2,1,0:T(2,128)}), f32[64,2,128]{2,1,0:T(2,128)S(1)}, u32[]{:S(2)}, u32[]{:S(2)}) async-start(f32[64,2,128]{2,1,0:T(2,128)} %bitcast), calls=%async_computation | async-start | bytes 131072 | tf_op jit(solution)/shard_map/all_to_all | solution.py:384
  30.3 0.0 copy-done.8
  30.3 0.0 copy-done.7
  30.3 0.0 copy-start.5
  30.3 0.0 copy-start.6
  30.3 0.2 copy.11.in_ref
  30.5 0.0 copy-done.1
  30.5 0.0 copy-done.2
  30.5 0.5 copy-done.5
  31.0 0.0 copy-done.6
  31.0 0.0 copy-start
  31.0 1.0 %copy-done = f32[320,320]{1,0:T(8,128)S(1)} copy-done((f32[320,320]{1,0:T(8,128)S(1)}, f32[320,320]{1,0:T(8,128)}, u32[]{:S(2)}) %copy-start) | copy-done | bytes 409624
  32.0 0.0 copy-start.3
  32.0 0.9 %copy-done.3 = bf16[320,96]{1,0:T(8,128)(2,1)S(1)} copy-done((bf16[320,96]{1,0:T(8,128)(2,1)S(1)}, bf16[320,96]{1,0:T(8,128)(2,1)}, u32[]{:S(2)}) %copy-start.3) | copy-done | bytes 61464
  32.9 2.1 %prepare.1 = (f32[2,320,128]{2,1,0:T(8,128)S(1)}, f32[2,16,128]{2,1,0:T(8,128)S(1)}, f32[2,2,128]{2,1,0:T(2,128)S(1)}, s32[8,128]{1,0:T(8,128)S(1)}, bf16[3,320,...) custom-call(s32[2]{0:T(128)S(1)} %copy-done.6, ...), custom_call_target="tpu_custom_call" | custom-call | tf_op jit(solution)/shard_map/prepare/pallas_call | solution.py:357
  35.0 5.2 %all-to-all-done = f32[64,2,128]{2,1,0:T(2,128)S(1)} async-done(((f32[64,2,128]{2,1,0:T(2,128)}), f32[64,2,128]{2,1,0:T(2,128)S(1)}, u32[]{:S(2)}, u32[]{:S(2)}) %all-to-all-start) | async-done | bytes 65568 | tf_op jit(solution)/shard_map/all_to_all | solution.py:384
  40.2 19.0 %picard.1 = (f32[128,128]{1,0:T(8,128)S(1)}, f32[128,128]{1,0:T(8,128)S(1)}) custom-call(f32[128,128]{1,0:T(8,128)S(1)} %bitcast.9, f32[2,320,128]{2,1,0:T(8,128)S(1)} %get-tuple-element.18.embed, f32[2,16,128]{2,1,0:T(8,128)S(1)} %get-tuple-element.19.bias, f32[2,2,128]{2,1,0:T(2,128)S(1)} %get-tuple-element.20.scales, ...), custom_call_target="tpu_custom_call" | custom-call | tf_op jit(solution)/shard_map/picard/pallas_call | solution.py:375
  59.2 1.6 %collective-permute-start.1 = (f32[128,128]{1,0:T(8,128)S(1)}, f32[128,128]{1,0:T(8,128)S(1)}, u32[]{:S(2)}, u32[]{:S(2)}) collective-permute-start(f32[128,128]{1,0:T(8,128)S(1)} %get-tuple-element.27), channel_id=1, source_target_pairs={{0,1},{1,0},{2,3},{3,2},{4,5},{5,4},{6,7},{7,6},{8,9},{9,8},{10,11... | collective-permute-start | bytes 196616 | tf_op jit(solution)/shard_map/ppermute | solution.py:379
  60.8 0.9 %collective-permute-done.1 = f32[128,128]{1,0:T(8,128)S(1)} collective-permute-done((f32[128,128]{1,0:T(8,128)S(1)}, f32[128,128]{1,0:T(8,128)S(1)}, u32[]{:S(2)}, u32[]{:S(2)}) %collective-permute-start.1) | collective-permute-done | bytes 65568 | tf_op jit(solution)/shard_map/ppermute | solution.py:379
  61.7 0.1 pad_maximum_fusion
  61.8 17.1 %all_to_all.10 = f32[64,4,128]{2,1,0:T(4,128)S(1)} all-to-all(f32[64,4,128]{2,1,0:T(4,128)S(1)} %pad_maximum_fusion), channel_id=1, replica_groups=mesh['groups'=2,'chips'=64,'cores'=2] {'chips'}, dimensions={0} | all-to-all | bytes 262144 | tf_op jit(solution)/shard_map/all_to_all | solution.py:384
  78.8 0.7 finish.1
  (1 shorter events, 0.0 us)
Async XLA Ops:
  0.6 29.9 %copy-start.1 = (bf16[320,320]{1,0:T(8,128)(2,1)S(1)}, bf16[320,320]{1,0:T(8,128)(2,1)}, u32[]{:S(2)}) copy-start(bf16[320,320]{1,0:T(8,128)(2,1)} %mid_ref.1) | copy-start | bytes 614404
  0.6 0.9 %copy-start.4 = (f32[1,4,4096]{2,1,0:T(4,128)S(1)}, f32[1,4,4096]{2,1,0:T(4,128)}, u32[]{:S(2)}) copy-start(f32[1,4,4096]{2,1,0:T(4,128)} %states_ref.1) | copy-start | bytes 196612
  1.6 21.4 %collective-permute-start = (f32[64,128]{1,0:T(8,128)S(1)}, f32[64,128]{1,0:T(8,128)S(1)}, u32[]{:S(2)}, u32[]{:S(2)}) collective-permute-start(f32[64,128]{1,0:T(8,128)S(1)} %get-tuple-element.17), channel_id=1, source_target_pairs={{0,1},{1,0},{2,3},{3,2},{4,5},{5,4},{6,7},{7,6},{8,9},{9,8},{10,11... | collective-permute-start | bytes 98312 | tf_op jit(solution)/shard_map/ppermute | solution.py:379
  23.0 7.3 %copy-start.8 = (s32[257]{0:T(512)S(1)}, s32[257]{0:T(512)}, u32[]{:S(2)}) copy-start(s32[257]{0:T(512)} %param.10) | copy-start | bytes 3088
  23.0 7.3 %copy-start.7 = (bf16[320,4]{0,1:T(4,128)(2,1)S(1)}, bf16[320,4]{0,1:T(4,128)(2,1)}, u32[]{:S(2)}) copy-start(bf16[320,4]{0,1:T(4,128)(2,1)} %param.12) | copy-start | bytes 7684
  23.7 6.8 %copy-start.2 = (bf16[384,96]{1,0:T(8,128)(2,1)S(1)}, bf16[384,96]{1,0:T(8,128)(2,1)}, u32[]{:S(2)}) copy-start(bf16[384,96]{1,0:T(8,128)(2,1)} %constant.4.clone.table_a_ref) | copy-start | bytes 221188
  23.7 16.5 %all-to-all-start = ((f32[64,2,128]{2,1,0:T(2,128)}), f32[64,2,128]{2,1,0:T(2,128)S(1)}, u32[]{:S(2)}, u32[]{:S(2)}) async-start(f32[64,2,128]{2,1,0:T(2,128)} %bitcast), calls=%async_computation | async-start | bytes 131072 | tf_op jit(solution)/shard_map/all_to_all | solution.py:384
  30.3 0.7 copy-start.5
  30.3 0.7 copy-start.6
  31.0 1.0 %copy-start = (f32[320,320]{1,0:T(8,128)S(1)}, f32[320,320]{1,0:T(8,128)}, u32[]{:S(2)}) copy-start(f32[320,320]{1,0:T(8,128)} %time_ref.1) | copy-start | bytes 1228804
  32.0 0.9 %copy-start.3 = (bf16[320,96]{1,0:T(8,128)(2,1)S(1)}, bf16[320,96]{1,0:T(8,128)(2,1)}, u32[]{:S(2)}) copy-start(bf16[320,96]{1,0:T(8,128)(2,1)} %constant.5.clone.table_b_ref) | copy-start | bytes 184324
  59.2 2.5 %collective-permute-start.1 = (f32[128,128]{1,0:T(8,128)S(1)}, f32[128,128]{1,0:T(8,128)S(1)}, u32[]{:S(2)}, u32[]{:S(2)}) collective-permute-start(f32[128,128]{1,0:T(8,128)S(1)} %get-tuple-element.27), channel_id=1, source_target_pairs={{0,1},{1,0},{2,3},{3,2},{4,5},{5,4},{6,7},{7,6},{8,9},{9,8},{10,11... | collective-permute-start | bytes 196616 | tf_op jit(solution)/shard_map/ppermute | solution.py:379
